TPU v7x, 32 devices: a whole 2x2x4 slice. The times are simulated.
32 devices in a mesh: dp: 16 (over z, y, core), space: 2 (over x).
Axes of the slice: x: 2, y: 2, z: 4, core: 2. Of those that a mesh axis runs over, the one named last changes fastest.
Arguments:
- feature_map: bfloat16 [16, 24, 84, 256], P('dp', 'space'), may hold values from -6 to 6
- proposals: int32 [16, 128, 4], P('dp'), may hold values from 0 to 84, as said below
- hidden_weight: bfloat16 [12544, 512], P(None, 'space'), may hold values from -0.0546875 to 0.0546875
- output_weight: bfloat16 [512, 512], P('space'), may hold values from -0.25 to 0.25
- upstream: bfloat16 [16, 128, 512], P('dp'), may hold values from -6 to 6
Outputs:
- hidden_weight_grad: float32 [12544, 512], P('dp', 'space')
- output_weight_grad: float32 [512, 512], P('space')
- feature_grad: float32 [16, 24, 84, 256], P('dp', 'space')
Inputs may be any that keep to these rules, and one draw needn't show every extreme that they name: `proposals`: each row holds top, left, bottom, right with top < bottom <= 24 and left < right <= 84.
All inputs are finite; a program needn't handle non-finite values.
Results may differ from a plain program's by a relative error of at most 0.012.
Values may be sent and summed in bfloat16 or wider, within the bound.
No kernel may reach another device: no remote copies, remote signals or barrier semaphores. Data moves between devices by JAX's collectives and lax.ppermute only.
A program may use at most 128 MiB of HBM per device.

v0:
```python
import jax
import jax.numpy as jnp
from jax import lax
from jax.sharding import PartitionSpec as P

POOL = 7


def axis_weights(low_edge, high_edge, grid_points):
    edge_start = low_edge.astype(jnp.float32)
    bin_size = (high_edge - low_edge).astype(jnp.float32) / POOL
    bin_index = jnp.arange(POOL).astype(jnp.float32)
    offsets = jnp.array([0.25, 0.75], jnp.float32)
    sample_points = (
        edge_start[:, None, None]
        + (bin_index[None, :, None] + offsets[None, None, :]) * bin_size[:, None, None]
        - 0.5
    )
    weights = jnp.maximum(
        0.0, 1.0 - jnp.abs(sample_points[..., None] - grid_points[None, None, None, :])
    )
    return jnp.mean(weights, axis=2)


def activate(values):
    return jax.nn.gelu(values, approximate=True)


def gelu_grad(values, incoming):
    return jax.vjp(activate, values)[1](incoming)[0]


def block_shape(proposal_count):
    block_size = 32
    return (block_size, proposal_count // block_size)


def crop_rows(own_map, row_weight, col_weight):
    height_cells, width_cells, channels = own_map.shape
    proposal_count = row_weight.shape[0]
    block_size, block_count = block_shape(proposal_count)
    flattened = jnp.transpose(own_map, (1, 0, 2)).reshape(width_cells, height_cells * channels)

    def per_block(blocks):
        row_part, col_part = blocks
        across = jnp.dot(
            col_part.reshape(block_size * POOL, width_cells),
            flattened,
            preferred_element_type=jnp.float32,
        )
        across = across.reshape(block_size, POOL, height_cells, channels)
        return jnp.einsum("riy,rjyc->rijc", row_part, across, precision=lax.Precision.HIGHEST)

    pooled = lax.map(
        per_block,
        (
            row_weight.reshape(block_count, block_size, POOL, height_cells),
            col_weight.reshape(block_count, block_size, POOL, width_cells),
        ),
    )
    return pooled.reshape(proposal_count, POOL * POOL * channels)


def crop_back(grad_pooled, row_weight, col_weight, channels):
    proposal_count, _, height_cells = row_weight.shape
    width_cells = col_weight.shape[2]
    block_size, block_count = block_shape(proposal_count)

    def per_block(running, blocks):
        row_part, col_part, grad_part = blocks
        grad_block = grad_part.reshape(block_size, POOL, POOL, channels)
        spread = jnp.einsum("riy,rijc->rjyc", row_part, grad_block, precision=lax.Precision.HIGHEST)
        added = lax.dot_general(
            col_part.astype(jnp.float32).reshape(block_size * POOL, width_cells),
            spread.reshape(block_size * POOL, height_cells * channels),
            (((0,), (0,)), ((), ())),
            precision=lax.Precision.HIGHEST,
            preferred_element_type=jnp.float32,
        )
        return (running + added, None)

    start = jnp.zeros((width_cells, height_cells * channels), jnp.float32)
    blocks = (
        row_weight.reshape(block_count, block_size, POOL, height_cells),
        col_weight.reshape(block_count, block_size, POOL, width_cells),
        grad_pooled.reshape(block_count, block_size, grad_pooled.shape[1]),
    )
    total, _ = lax.scan(per_block, start, blocks)
    return jnp.transpose(total.reshape(width_cells, height_cells, channels), (1, 0, 2))


def on_device(feature_map, proposals, hidden_weight, output_weight, upstream):
    own_map = feature_map[0]
    corners = proposals[0]
    own_height = own_map.shape[0]
    map_width = own_map.shape[1]
    channels = own_map.shape[2]
    row_offset = lax.axis_index("space") * own_height
    local_grid = (row_offset + jnp.arange(own_height, dtype=jnp.int32)).astype(jnp.float32)
    row_weight = axis_weights(corners[:, 0], corners[:, 2], local_grid)
    col_weight = axis_weights(
        corners[:, 1], corners[:, 3], jnp.arange(map_width, dtype=jnp.int32).astype(jnp.float32)
    ).astype(jnp.bfloat16)
    full_grid = jnp.arange(own_height * lax.axis_size("space"), dtype=jnp.int32).astype(jnp.float32)
    full_weight = axis_weights(corners[:, 0], corners[:, 2], full_grid)
    whole_map = lax.all_gather(own_map, "space", axis=0, tiled=True)
    pooled = crop_rows(whole_map, full_weight, col_weight).astype(jnp.bfloat16)
    pre_hidden = jnp.dot(pooled, hidden_weight, preferred_element_type=jnp.float32)
    hidden = activate(pre_hidden).astype(jnp.bfloat16)
    pre_output = lax.psum(
        jnp.dot(hidden, output_weight, preferred_element_type=jnp.float32).astype(jnp.bfloat16),
        "space",
    ).astype(jnp.float32)
    output_delta = gelu_grad(pre_output, upstream[0].astype(jnp.float32)).astype(jnp.bfloat16)
    step_second = lax.dot_general(
        hidden, output_delta, (((0,), (0,)), ((), ())), preferred_element_type=jnp.float32
    )
    second_total = lax.psum(step_second, "dp")
    hidden_back = lax.dot_general(
        output_delta, output_weight, (((1,), (1,)), ((), ())), preferred_element_type=jnp.float32
    )
    hidden_delta = gelu_grad(pre_hidden, hidden_back).astype(jnp.bfloat16)
    column_rows = lax.all_to_all(pooled, "dp", split_axis=1, concat_axis=0, tiled=True)
    delta_rows = lax.all_gather(hidden_delta, "dp", axis=0, tiled=True)
    first_total = lax.dot_general(
        column_rows, delta_rows, (((0,), (0,)), ((), ())), preferred_element_type=jnp.float32
    )
    partial_grad = lax.dot_general(
        hidden_delta, hidden_weight, (((1,), (1,)), ((), ())), preferred_element_type=jnp.float32
    )
    grad_share = lax.psum_scatter(
        partial_grad.astype(jnp.bfloat16), "space", scatter_dimension=0, tiled=True
    ).astype(jnp.float32)
    pooled_grad = lax.all_gather(
        grad_share.astype(jnp.bfloat16), "space", axis=0, tiled=True
    ).astype(grad_share.dtype)
    map_grad = crop_back(pooled_grad, row_weight, col_weight, channels)
    return (first_total, second_total, map_grad[None])


def solution(mesh):
    placed = (
        P("dp", "space", None, None),
        P("dp", None, None),
        P(None, "space"),
        P("space", None),
        P("dp", None, None),
    )
    return jax.shard_map(
        on_device,
        mesh=mesh,
        in_specs=placed,
        out_specs=(P("dp", "space"), P("space", None), P("dp", "space", None, None)),
        check_vma=False,
    )
```

profile of v0, /device:TPU:0, one launch (start us, length us, event | category | flops | bytes accessed | tf_op | source)
XLA Modules:
  0.0 361.1 jit_solution(6747203176717695255)
XLA Ops:
  7.2 0.8 convert_bitcast_fusion
  8.0 0.8 multiply_bitcast_fusion
  8.9 0.7 broadcast_add_fusion
  9.7 1.0 maximum_reduce_fusion
  11.3 16.2 %all-gather = bf16[1,24,84,256]{3,2,0,1:T(8,128)(2,1)S(1)} all-gather(bf16[1,12,84,256]{3,2,0,1:T(8,128)(2,1)} %bitcast.120), channel_id=2, replica_groups=mesh['dp'=16,'space'=2] {'space'}, dimensions={1}, use_global_device_ids=true | all-gather | bytes 1548288 | tf_op jit(solution)/shard_map/all_gather | solution.py:106
  28.0 34.6 %while.21 = (s32[]{:T(128)}, bf16[4,32,7,7,256]{4,2,3,1,0:T(8,128)(2,1)}, f32[4,32,7,24]{3,2,1,0:T(8,128)S(1)}, bf16[4,32,7,84]{3,1,0,2:T(8,128)(2,1)S(1)}, bf16[84,6144]{1,0:T(8,128)(2,1)S(1)}, /*index=5*/s32[]{:T(128)}) while((s32[]{:T(128)}, bf16[4,32,7,7,256]{4,2,3,1,0:T(8,128)(2,1)}, f32[4,32,7,24]{3,2,1,0:T(8,128)S(1)}, ...), condition=%wide.region_3.4_spmd, body=%wide.region_2.0_spmd.sunk | while | flops 346816512 | bytes 18293832 | solution.py:54
  28.3 0.9 fusion.66
  29.2 7.5 %bitcast_dynamic-update-slice_fusion.2 = bf16[4,32,7,7,256]{4,2,3,1,0:T(8,128)(2,1)} fusion(bf16[4,32,7,7,256]{4,2,3,1,0:T(8,128)(2,1)} %get-tuple-element.230, s32[]{:T(128)} %get-tuple-element.229, f32[32,7,24,256]{3,0,2,1:T(8,128)S(1)} %fusion.66, f32[4,32,7,24]{3,2,1,0:T(8,128)S(1)} %get-tuple-element.237), kind=kOutput, calls=%fused_computation.2.clone.1 | convolution fusion | flops 115605504 | bytes 7472128 | tf_op jit(solution)/shard_map/while/body/eval_jaxpr/riy,rjyc->rijc/dot_general | solution.py:52
  37.0 0.9 fusion.66
  37.8 7.5 %bitcast_dynamic-update-slice_fusion.2 = bf16[4,32,7,7,256]{4,2,3,1,0:T(8,128)(2,1)} fusion(bf16[4,32,7,7,256]{4,2,3,1,0:T(8,128)(2,1)} %get-tuple-element.230, s32[]{:T(128)} %get-tuple-element.229, f32[32,7,24,256]{3,0,2,1:T(8,128)S(1)} %fusion.66, f32[4,32,7,24]{3,2,1,0:T(8,128)S(1)} %get-tuple-element.237), kind=kOutput, calls=%fused_computation.2.clone.1 | convolution fusion | flops 115605504 | bytes 7472128 | tf_op jit(solution)/shard_map/while/body/eval_jaxpr/riy,rjyc->rijc/dot_general | solution.py:52
  45.7 0.9 fusion.66
  46.5 7.5 %bitcast_dynamic-update-slice_fusion.2 = bf16[4,32,7,7,256]{4,2,3,1,0:T(8,128)(2,1)} fusion(bf16[4,32,7,7,256]{4,2,3,1,0:T(8,128)(2,1)} %get-tuple-element.230, s32[]{:T(128)} %get-tuple-element.229, f32[32,7,24,256]{3,0,2,1:T(8,128)S(1)} %fusion.66, f32[4,32,7,24]{3,2,1,0:T(8,128)S(1)} %get-tuple-element.237), kind=kOutput, calls=%fused_computation.2.clone.1 | convolution fusion | flops 115605504 | bytes 7472128 | tf_op jit(solution)/shard_map/while/body/eval_jaxpr/riy,rjyc->rijc/dot_general | solution.py:52
  54.3 0.9 fusion.66
  55.2 7.5 %bitcast_dynamic-update-slice_fusion.2 = bf16[4,32,7,7,256]{4,2,3,1,0:T(8,128)(2,1)} fusion(bf16[4,32,7,7,256]{4,2,3,1,0:T(8,128)(2,1)} %get-tuple-element.230, s32[]{:T(128)} %get-tuple-element.229, f32[32,7,24,256]{3,0,2,1:T(8,128)S(1)} %fusion.66, f32[4,32,7,24]{3,2,1,0:T(8,128)S(1)} %get-tuple-element.237), kind=kOutput, calls=%fused_computation.2.clone.1 | convolution fusion | flops 115605504 | bytes 7472128 | tf_op jit(solution)/shard_map/while/body/eval_jaxpr/riy,rjyc->rijc/dot_general | solution.py:52
  62.6 5.1 %copy.77 = bf16[4,32,7,7,256]{4,3,2,1,0:T(8,128)(2,1)} copy(bf16[4,32,7,7,256]{4,2,3,1,0:T(8,128)(2,1)} %get-tuple-element.57) | data formatting | bytes 6422528 | tf_op jit(solution)/shard_map/convert_element_type | solution.py:107
  67.8 5.6 %convert_element_type.132 = bf16[128,12544]{1,0:T(8,128)(2,1)S(1)} reshape(bf16[4,32,7,7,256]{4,3,2,1,0:T(8,128)(2,1)} %copy.77) | data formatting | bytes 6422528 | tf_op jit(solution)/shard_map/convert_element_type | solution.py:107
  73.4 3.8 %fusion.39 = f32[128,256]{1,0:T(8,128)S(1)} fusion(bf16[128,12544]{1,0:T(8,128)(2,1)S(1)} %convert_element_type.132, bf16[12544,256]{1,0:T(8,128)(2,1)} %param.14), kind=kOutput, calls=%fused_computation.69 | convolution fusion | flops 822083584 | bytes 9764864 | tf_op jit(solution)/shard_map/dot_general | solution.py:108
  77.2 0.6 copy-done.4
  77.9 0.9 convolution_convert_fusion.1
  79.0 22.9 %all-reduce.3.cloned.1.call-done = bf16[128,512]{1,0:T(8,128)(2,1)} async-done(((bf16[128,512]{1,0:T(8,128)(2,1)}), bf16[128,512]{1,0:T(8,128)(2,1)}) %all-reduce.3.cloned.1.call-update) | async-done | bytes 131088 | tf_op jit(solution)/shard_map/psum | solution.py:110
  101.9 1.2 fusion.24
  103.1 0.6 copy-done.6
  103.7 1.1 fusion.37
  104.9 6.8 %convolution_convert_fusion = bf16[128,12544]{1,0:T(8,128)(2,1)} fusion(bf16[128,256]{1,0:T(8,128)(2,1)S(1)} %fusion.37, bf16[12544,256]{1,0:T(8,128)(2,1)} %param.14), kind=kOutput, calls=%fused_computation.21 | convolution fusion | flops 823689216 | bytes 9699328 | tf_op jit(solution)/shard_map/dot_general | solution.py:128
  111.7 9.3 %convert_element_type.129 = bf16[128,16,784]{2,1,0:T(8,128)(2,1)} reshape(bf16[4,32,7,7,256]{4,3,2,1,0:T(8,128)(2,1)} %copy.77) | data formatting | bytes 6422528 | tf_op jit(solution)/shard_map/convert_element_type | solution.py:107
  121.0 6.2 %copy.78 = bf16[128,16,784]{0,2,1:T(8,128)(2,1)} copy(bf16[128,16,784]{2,1,0:T(8,128)(2,1)} %convert_element_type.129) | data formatting | bytes 6422528 | tf_op jit(solution)/shard_map/convert_element_type | solution.py:107
  127.2 5.8 %all-to-all-start = ((bf16[128,16,784]{0,2,1:T(8,128)(2,1)}), bf16[128,16,784]{0,2,1:T(8,128)(2,1)S(1)}, u32[]{:S(2)}, u32[]{:S(2)}) async-start(bf16[128,16,784]{0,2,1:T(8,128)(2,1)} %copy.78), calls=%async_computation | async-start | bytes 6422528 | tf_op jit(solution)/shard_map/all_to_all | solution.py:123
  133.0 0.7 all-gather.4.cloned.1.call-update
  133.8 22.2 %reduce-scatter.2.cloned.1.call-done = bf16[64,12544]{1,0:T(8,128)(2,1)} async-done(((bf16[128,12544]{1,0:T(8,128)(2,1)}), bf16[64,12544]{1,0:T(8,128)(2,1)}) %reduce-scatter.2.cloned.1.call-update) | async-done | bytes 1605648 | tf_op jit(solution)/shard_map/reduce_scatter | solution.py:131
  156.1 0.9 copy.89
  157.2 1.0 copy.90
  158.2 2.0 fusion.38
  160.2 50.5 %all-gather.4.cloned.1.call-done = bf16[2048,256]{1,0:T(8,128)(2,1)} async-done(((bf16[128,256]{1,0:T(8,128)(2,1)}), bf16[2048,256]{1,0:T(8,128)(2,1)}) %all-gather.4.cloned.1.call-update) | async-done | bytes 1048592 | tf_op jit(solution)/shard_map/all_gather | solution.py:124
  210.8 3.1 fusion.18
  213.9 44.3 %all-gather.6.cloned.1.call-done = bf16[128,12544]{1,0:T(8,128)(2,1)} async-done(((bf16[64,12544]{1,0:T(8,128)(2,1)}), bf16[128,12544]{1,0:T(8,128)(2,1)}) %all-gather.6.cloned.1.call-update) | async-done | bytes 3211280 | tf_op jit(solution)/shard_map/all_gather | solution.py:134
  258.2 5.1 %convert.3 = f32[4,32,12544]{2,1,0:T(8,128)} convert(bf16[4,32,12544]{2,1,0:T(8,128)(2,1)} %bitcast.115) | non-fusion elementwise | flops 1605632 | bytes 9633792 | tf_op jit(solution)/shard_map/reshape | solution.py:86
  263.3 51.9 %while.22 = (s32[]{:T(128)}, f32[84,3072]{1,0:T(8,128)}, bf16[4,32,7,84]{3,2,1,0:T(8,128)(2,1)}, f32[4,32,12544]{2,1,0:T(8,128)}, f32[4,32,7,12]{3,2,1,0:T(8,128)}, /*index=5*/s32[]{:T(128)}, s32[]{:T(128)}) while((s32[]{:T(128)}, f32[84,3072]{1,0:T(8,128)}, bf16[4,32,7,84]{3,2,1,0:T(8,128)(2,1)}, f32[4,32,12544]{2,1,0:T(8,128)}, ...), condition=%wide.region_9.10_spmd.clone, body=%wide.region_8.9_spmd.clone.sunk | while | flops 751951872 | bytes 21422432 | solution.py:88
  263.3 1.5 constant_dynamic-slice_fusion.5
  264.8 0.4 reshape.239
  265.3 4.5 %fusion.71 = f32[32,7,256,12]{2,3,1,0:T(8,128)S(1)} fusion(f32[32,7,7,256]{3,2,1,0:T(8,128)S(1)} %reshape.239, f32[4,32,7,12]{3,2,1,0:T(8,128)} %get-tuple-element.259, s32[]{:T(128)} %get-tuple-element.248), kind=kOutput, calls=%fused_computation.14.clone.1 | convolution fusion | flops 57802752 | bytes 4489728 | tf_op jit(solution)/shard_map/while/body/eval_jaxpr/riy,rijc->rjyc/dot_general | solution.py:72
  269.8 2.4 copy.120
  272.2 0.9 constant_dynamic-slice_fusion.4
  273.1 2.2 convolution_add_fusion.2
  275.3 1.5 constant_dynamic-slice_fusion.5
  276.9 0.4 reshape.239
  277.3 4.5 %fusion.71 = f32[32,7,256,12]{2,3,1,0:T(8,128)S(1)} fusion(f32[32,7,7,256]{3,2,1,0:T(8,128)S(1)} %reshape.239, f32[4,32,7,12]{3,2,1,0:T(8,128)} %get-tuple-element.259, s32[]{:T(128)} %get-tuple-element.248), kind=kOutput, calls=%fused_computation.14.clone.1 | convolution fusion | flops 57802752 | bytes 4489728 | tf_op jit(solution)/shard_map/while/body/eval_jaxpr/riy,rijc->rjyc/dot_general | solution.py:72
  281.8 2.4 copy.120
  284.3 0.9 constant_dynamic-slice_fusion.4
  285.1 3.5 convolution_add_fusion.2
  288.6 1.5 constant_dynamic-slice_fusion.5
  290.1 0.4 reshape.239
  290.6 4.5 %fusion.71 = f32[32,7,256,12]{2,3,1,0:T(8,128)S(1)} fusion(f32[32,7,7,256]{3,2,1,0:T(8,128)S(1)} %reshape.239, f32[4,32,7,12]{3,2,1,0:T(8,128)} %get-tuple-element.259, s32[]{:T(128)} %get-tuple-element.248), kind=kOutput, calls=%fused_computation.14.clone.1 | convolution fusion | flops 57802752 | bytes 4489728 | tf_op jit(solution)/shard_map/while/body/eval_jaxpr/riy,rijc->rjyc/dot_general | solution.py:72
  295.1 2.4 copy.120
  297.5 0.9 constant_dynamic-slice_fusion.4
  298.4 3.5 convolution_add_fusion.2
  301.9 1.5 constant_dynamic-slice_fusion.5
  303.9 4.5 %fusion.71 = f32[32,7,256,12]{2,3,1,0:T(8,128)S(1)} fusion(f32[32,7,7,256]{3,2,1,0:T(8,128)S(1)} %reshape.239, f32[4,32,7,12]{3,2,1,0:T(8,128)} %get-tuple-element.259, s32[]{:T(128)} %get-tuple-element.248), kind=kOutput, calls=%fused_computation.14.clone.1 | convolution fusion | flops 57802752 | bytes 4489728 | tf_op jit(solution)/shard_map/while/body/eval_jaxpr/riy,rijc->rjyc/dot_general | solution.py:72
  308.4 2.4 copy.120
  310.8 0.9 constant_dynamic-slice_fusion.4
  311.7 3.5 convolution_add_fusion.2
  315.2 1.6 reshape.224
  316.8 2.0 copy.84
  318.8 33.9 %all-reduce.5.cloned.1.call-done = f32[256,512]{1,0:T(8,128)} async-done(((f32[256,512]{1,0:T(8,128)}), f32[256,512]{1,0:T(8,128)}) %all-reduce.5.cloned.1.call-update) | async-done | bytes 524304 | tf_op jit(solution)/shard_map/psum | solution.py:118
  352.7 1.9 copy.136
  (54 shorter events, 3.7 us)
Async XLA Ops:
  7.2 70.7 %copy-start = (bf16[256,512]{1,0:T(8,128)(2,1)S(1)}, bf16[256,512]{1,0:T(8,128)(2,1)}, u32[]{:S(2)}) copy-start(bf16[256,512]{1,0:T(8,128)(2,1)} %param.15) | copy-start | bytes 786436
  7.2 94.7 %all-reduce.3.cloned.1.call-start = ((), (), s32[]{:S(2)}) async-start(), calls=%async_computation.2 | async-start | bytes 262144 | tf_op jit(solution)/shard_map/psum | solution.py:110
  10.7 17.0 %copy-start.2 = (bf16[128,7,84]{0,2,1:T(8,128)(2,1)}, bf16[128,7,84]{0,2,1:T(8,128)(2,1)S(1)}, u32[]{:S(2)}) copy-start(bf16[128,7,84]{0,2,1:T(8,128)(2,1)S(1)} %multiply_convert_fusion) | copy-start | bytes 451588
  77.2 0.7 copy-start.4
  78.7 77.3 %reduce-scatter.2.cloned.1.call-start = ((), (), s32[]{:S(2)}) async-start(), calls=%async_computation.5 | async-start | bytes 4816896 | tf_op jit(solution)/shard_map/reduce_scatter | solution.py:131
  103.0 0.6 copy-start.6
  104.8 6.8 %copy-start.7 = (bf16[128,256]{1,0:T(8,128)(2,1)}, bf16[128,256]{1,0:T(8,128)(2,1)S(1)}, u32[]{:S(2)}) copy-start(bf16[128,256]{1,0:T(8,128)(2,1)S(1)} %fusion.37) | copy-start | bytes 196612
  127.2 28.8 %copy-start.3 = (bf16[128,7,84]{0,2,1:T(8,128)(2,1)S(1)}, bf16[128,7,84]{0,2,1:T(8,128)(2,1)}, u32[]{:S(2)}) copy-start(bf16[128,7,84]{0,2,1:T(8,128)(2,1)} %copy-done.2) | copy-start | bytes 451588
  127.2 31.0 %copy-start.5 = (f32[128,256]{1,0:T(8,128)S(1)}, f32[128,256]{1,0:T(8,128)}, u32[]{:S(2)}) copy-start(f32[128,256]{1,0:T(8,128)} %copy-done.4) | copy-start | bytes 393220
  127.2 83.6 %all-to-all-start = ((bf16[128,16,784]{0,2,1:T(8,128)(2,1)}), bf16[128,16,784]{0,2,1:T(8,128)(2,1)S(1)}, u32[]{:S(2)}, u32[]{:S(2)}) async-start(bf16[128,16,784]{0,2,1:T(8,128)(2,1)} %copy.78), calls=%async_computation | async-start | bytes 6422528 | tf_op jit(solution)/shard_map/all_to_all | solution.py:123
  133.0 77.8 %all-gather.4.cloned.1.call-start = ((), (), s32[]{:S(2)}) async-start(), calls=%async_computation.3 | async-start | bytes 1114112 | tf_op jit(solution)/shard_map/all_gather | solution.py:124
  133.7 124.4 %all-gather.6.cloned.1.call-start = ((), (), s32[]{:S(2)}) async-start(), calls=%async_computation.6 | async-start | bytes 4816896 | tf_op jit(solution)/shard_map/all_gather | solution.py:134
  156.0 196.7 %all-reduce.5.cloned.1.call-start = ((), (), s32[]{:S(2)}) async-start(), calls=%async_computation.4 | async-start | bytes 1048576 | tf_op jit(solution)/shard_map/psum | solution.py:118
  315.2 39.4 %copy-start.1 = (bf16[256,512]{1,0:T(8,128)(2,1)S(1)}, bf16[256,512]{1,0:T(8,128)(2,1)}, u32[]{:S(2)}) copy-start(bf16[256,512]{1,0:T(8,128)(2,1)} %param.15) | copy-start | bytes 786436
Sparse Core Ops, SparseCore 0:
  78.9 22.9 all-reduce.2
  111.8 44.1 reduce-scatter.1
  158.2 52.5 all-gather.3
  212.2 45.9 all-gather.5
  262.0 90.6 all-reduce.4
where the time goes:
time: 363 us; the launch traced here: 361 us
  waiting for transfers between devices  175 us (48%)
  matrix products  81.6 us (22%)
  local copies, waits for them, and re-layouts  58.4 us (16%)
  blocking collectives  16.2 us (4%)
  between operations  14 us (4%)
  other arithmetic  10.1 us (3%)
  starting transfers between devices  6.13 us (2%)
    all_gather x1, waiting for transfers between devices, on_device(): delta_rows = lax.all_gather(hidden_delta, 'dp', axis=0, tiled=True)  50.5 us
    all_gather x1, waiting for transfers between devices, on_device(): lax.all_gather(grad_share.astype(jnp.bfloat16), 'space', axis=0, tiled=True)  44.3 us
    psum x1, waiting for transfers between devices, on_device(): second_total = lax.psum(step_second, 'dp')  33.9 us
    dot_general x4, matrix products, per_block(): jnp.einsum('riy,rjyc->rijc', row_part, across, precision=lax.Precision.HI...  29.9 us
    convert_element_type x4, local copies, waits for them, and re-layouts, on_device(): pooled = crop_rows(whole_map, full_weight, col_weight).astype(jnp.bfloat16)  26.3 us
    psum x1, waiting for transfers between devices, on_device(): lax.psum(jnp.dot(hidden, output_weight, preferred_element_type=jnp.float3...  22.9 us
    reduce_scatter x1, waiting for transfers between devices, on_device(): lax.psum_scatter(partial_grad.astype(jnp.bfloat16), 'space', scatter_dime...  22.2 us
    dot_general x4, matrix products, per_block(): jnp.einsum('riy,rijc->rjyc', row_part, grad_block, precision=lax.Precisio...  17.9 us
  transfers between devices with their start and end apart: 6, of which 5 were waited for; matrix products, arithmetic and copies ran while one was open for 23% of the time, Pallas kernels for 0%

commit v1 on v0

v1 whole, which is shorter than its diff:
```python
import jax
import jax.numpy as jnp
from jax import lax
from jax.experimental import pallas as pl
from jax.experimental.pallas import tpu as pltpu
from jax.sharding import PartitionSpec as P

POOL = 7
BINS = POOL * POOL
F32 = jnp.float32
BF16 = jnp.bfloat16


def activate(values):
    return jax.nn.gelu(values, approximate=True)


def gelu_grad(values, incoming):
    return jax.vjp(activate, values)[1](incoming)[0]


def sample_points(low_edge, high_edge):
    edge_start = low_edge.astype(F32)
    bin_size = (high_edge - low_edge).astype(F32) / POOL
    bin_index = jnp.arange(POOL).astype(F32)
    return [
        edge_start[None, :] + (bin_index[:, None] + offset) * bin_size[None, :] - 0.5
        for offset in (0.25, 0.75)
    ]


def tent(points, grid):
    return 0.5 * (
        jnp.maximum(0.0, 1.0 - jnp.abs(points[0] - grid))
        + jnp.maximum(0.0, 1.0 - jnp.abs(points[1] - grid))
    )


def dot(a, b, dims=((1,), (0,))):
    return lax.dot_general(a, b, (dims, ((), ())), preferred_element_type=F32)


def params(grid_rank, **more):
    return pltpu.CompilerParams(
        dimension_semantics=("arbitrary",) * grid_rank, vmem_limit_bytes=60 * 2**20, **more
    )


def crop_forward(row_tab, col_tab, map_own, map_other, weight, owners):
    _, rois, cells = row_tab.shape
    half_cells, channels = map_own.shape
    hidden = weight.shape[1]
    half = rois // 2
    owned = BINS * channels // owners
    part = owned // 2
    aligned = owned % 16 == 0

    def body(row_ref, col_ref, own_ref, other_ref, weight_ref, eye_ref, pre_ref, pack_ref, w2, crops_t):
        i = pl.program_id(0)
        row = row_ref[0]
        for j in range(POOL):
            w2[j * rois : (j + 1) * rois, :] = row * col_ref[j]
        pooled = (
            dot(w2[:, :half_cells], own_ref[...]) + dot(w2[:, half_cells:], other_ref[...])
        ).astype(BF16)
        acc = jnp.zeros((rois, hidden), F32)
        for j in range(POOL):
            crop = pooled[j * rois : (j + 1) * rois]
            acc += dot(crop, weight_ref[j * channels : (j + 1) * channels, :])
            twice = jnp.concatenate([crop[:half], crop[:half]], axis=0)
            start = pl.multiple_of((i * POOL + j) * channels, channels)
            crops_t[pl.ds(start, channels), :] = dot(eye_ref[...], twice, ((1,), (1,)))

        @pl.when(i == 0)
        def _():
            pre_ref[...] = acc

        @pl.when(i > 0)
        def _():
            pre_ref[...] += acc

        if not aligned:
            start = pl.multiple_of(i * (POOL * channels), channels)
            pack_ref[...] = crops_t[pl.ds(start, POOL * channels), :].astype(BF16)
            return

        @pl.when(i == POOL - 1)
        def _():
            left = lax.broadcasted_iota(jnp.int32, (part, 2 * half), 1) < half

            def pack(e, carry):
                start = pl.multiple_of(e * owned, 8)
                first = crops_t[pl.ds(start, part), :]
                second = crops_t[pl.ds(start + part, part), :]
                pack_ref[e] = jnp.where(left, first, second).astype(BF16)
                return carry

            lax.fori_loop(0, owners, pack, 0)

    whole = lambda *shape: pl.BlockSpec(shape, lambda i: (0,) * len(shape))
    if aligned:
        pack_spec, pack_shape = whole(owners, part, 2 * half), (owners, part, 2 * half)
    else:
        pack_spec = pl.BlockSpec((POOL * channels, 2 * half), lambda i: (i, 0))
        pack_shape = (BINS * channels, 2 * half)
    pre_hidden, packed = pl.pallas_call(
        body,
        grid=(POOL,),
        in_specs=[
            pl.BlockSpec((1, rois, cells), lambda i: (i, 0, 0)),
            whole(POOL, rois, cells),
            whole(half_cells, channels),
            whole(half_cells, channels),
            pl.BlockSpec((POOL * channels, hidden), lambda i: (i, 0)),
            whole(channels, channels),
        ],
        out_specs=[whole(rois, hidden), pack_spec],
        out_shape=[
            jax.ShapeDtypeStruct((rois, hidden), F32),
            jax.ShapeDtypeStruct(pack_shape, BF16),
        ],
        scratch_shapes=[
            pltpu.VMEM((POOL * rois, cells), BF16),
            pltpu.VMEM((BINS * channels, 2 * half), F32),
        ],
        compiler_params=params(1),
        cost_estimate=pl.CostEstimate(
            flops=2 * BINS * rois * cells * channels, transcendentals=0, bytes_accessed=20 * 2**20
        ),
        name="crop_forward",
    )(row_tab, col_tab, map_own, map_other, weight, jnp.eye(channels, dtype=BF16))
    if not aligned:
        packed = packed[:, :half].reshape(owners, owned, half)
    return pre_hidden, packed


def head(pre_own, pre_received, out_own, out_other, upstream):
    rois, hidden = pre_own.shape
    outputs = out_own.shape[1]
    half = rois // 2

    def body(own_ref, recv_ref, wown_ref, wother_ref, up_ref, hd_ref, mine_ref, grad_ref):
        pre_a = own_ref[...]
        pre_b = jnp.concatenate([recv_ref[half:], recv_ref[:half]], axis=0).astype(F32)
        hid_a = activate(pre_a).astype(BF16)
        hid_b = activate(pre_b).astype(BF16)
        pre_output = dot(hid_a, wown_ref[...]) + dot(hid_b, wother_ref[...])
        delta = gelu_grad(pre_output, up_ref[...].astype(F32)).astype(BF16)
        grad_ref[...] = dot(hid_a, delta, ((0,), (0,)))
        hd_a = gelu_grad(pre_a, dot(delta, wown_ref[...], ((1,), (1,)))).astype(BF16)
        hd_b = gelu_grad(
            pre_b[:half], dot(delta[:half], wother_ref[...], ((1,), (1,)))
        ).astype(BF16)
        hd_ref[...] = hd_a
        mine_ref[:, :hidden] = hd_a[:half]
        mine_ref[:, hidden:] = hd_b

    return pl.pallas_call(
        body,
        out_shape=[
            jax.ShapeDtypeStruct((rois, hidden), BF16),
            jax.ShapeDtypeStruct((half, 2 * hidden), BF16),
            jax.ShapeDtypeStruct((hidden, outputs), F32),
        ],
        compiler_params=pltpu.CompilerParams(vmem_limit_bytes=32 * 2**20),
        cost_estimate=pl.CostEstimate(flops=2 * 10**9, transcendentals=0, bytes_accessed=2**21),
        name="head",
    )(pre_own, pre_received, out_own, out_other, upstream)


def crop_backward_other(row_tab, col_tab, delta, weight):
    _, cells, rois = row_tab.shape
    hidden = weight.shape[1]
    channels = weight.shape[0] // BINS
    half_cells = cells // 2

    def body(row_ref, col_ref, delta_ref, weight_ref, crop_ref, out_ref, w2, acc):
        i = pl.program_id(0)
        row = row_ref[0]
        for j in range(POOL):
            w2[:, j * rois : (j + 1) * rois] = row * col_ref[j]
            crop_ref[j * rois : (j + 1) * rois, :] = dot(
                delta_ref[...], weight_ref[j * channels : (j + 1) * channels, :], ((1,), (1,))
            ).astype(BF16)
        part = dot(w2[...], crop_ref[...])

        @pl.when(i == 0)
        def _():
            acc[...] = part

        @pl.when(i > 0)
        def _():
            acc[...] += part

        @pl.when(i == POOL - 1)
        def _():
            out_ref[...] = acc[...].astype(BF16)

    return pl.pallas_call(
        body,
        grid=(POOL,),
        in_specs=[
            pl.BlockSpec((1, half_cells, rois), lambda i: (i, 1, 0)),
            pl.BlockSpec((POOL, half_cells, rois), lambda i: (0, 1, 0)),
            pl.BlockSpec((rois, hidden), lambda i: (0, 0)),
            pl.BlockSpec((POOL * channels, hidden), lambda i: (i, 0)),
        ],
        out_specs=[
            pl.BlockSpec((POOL * rois, channels), lambda i: (i, 0)),
            pl.BlockSpec((half_cells, channels), lambda i: (0, 0)),
        ],
        out_shape=[
            jax.ShapeDtypeStruct((BINS * rois, channels), BF16),
            jax.ShapeDtypeStruct((half_cells, channels), BF16),
        ],
        scratch_shapes=[
            pltpu.VMEM((half_cells, POOL * rois), BF16),
            pltpu.VMEM((half_cells, channels), F32),
        ],
        compiler_params=params(1),
        cost_estimate=pl.CostEstimate(
            flops=BINS * rois * cells * channels, transcendentals=0, bytes_accessed=14 * 2**20
        ),
        name="crop_backward_other",
    )(row_tab, col_tab, delta, weight)


def crop_backward_own(row_tab, col_tab, crops):
    _, cells, rois = row_tab.shape
    channels = crops.shape[1]
    half_cells = cells // 2

    def body(row_ref, col_ref, crop_ref, out_ref, w2):
        i = pl.program_id(0)
        row = row_ref[0]
        for j in range(POOL):
            w2[:, j * rois : (j + 1) * rois] = row * col_ref[j]
        part = dot(w2[...], crop_ref[...])

        @pl.when(i == 0)
        def _():
            out_ref[...] = part

        @pl.when(i > 0)
        def _():
            out_ref[...] += part

    return pl.pallas_call(
        body,
        grid=(POOL,),
        in_specs=[
            pl.BlockSpec((1, half_cells, rois), lambda i: (i, 0, 0)),
            pl.BlockSpec((POOL, half_cells, rois), lambda i: (0, 0, 0)),
            pl.BlockSpec((POOL * rois, channels), lambda i: (i, 0)),
        ],
        out_specs=pl.BlockSpec((half_cells, channels), lambda i: (0, 0)),
        out_shape=jax.ShapeDtypeStruct((half_cells, channels), F32),
        scratch_shapes=[pltpu.VMEM((half_cells, POOL * rois), BF16)],
        compiler_params=params(1),
        cost_estimate=pl.CostEstimate(
            flops=BINS * rois * cells * channels, transcendentals=0, bytes_accessed=9 * 2**20
        ),
        name="crop_backward_own",
    )(row_tab, col_tab, crops)


def weight_grad(packed, deltas, order, me):
    images, part, lanes = packed.shape
    half, width = deltas.shape[1:]
    hidden = width // 2
    if lanes == half:
        place = jnp.array([order[m] for m in range(images)])
        in_order = deltas[place[jnp.arange(images) ^ me]]
        total = jnp.einsum("mpr,mrh->ph", packed, in_order, preferred_element_type=F32)
        return total[:, :hidden], total[:, hidden:].astype(BF16)

    def body(me_ref, packed_ref, delta_ref, own_ref, other_ref):
        left = lax.broadcasted_iota(jnp.int32, (part, lanes), 1) < half
        tops = jnp.zeros((part, width), F32)
        bottoms = jnp.zeros((part, width), F32)
        for m in range(0, images, 2):
            a = packed_ref[me_ref[0] ^ m]
            b = packed_ref[me_ref[0] ^ (m + 1)]
            pair = jnp.concatenate([delta_ref[order[m]], delta_ref[order[m + 1]]], axis=0)
            a, b = a.astype(F32), b.astype(F32)
            top = jnp.where(left, a, pltpu.roll(b, half, 1)).astype(BF16)
            bottom = jnp.where(left, pltpu.roll(a, half, 1), b).astype(BF16)
            tops += dot(top, pair)
            bottoms += dot(bottom, pair)
        own_ref[:part] = tops[:, :hidden]
        own_ref[part:] = bottoms[:, :hidden]
        other_ref[:part] = tops[:, hidden:].astype(BF16)
        other_ref[part:] = bottoms[:, hidden:].astype(BF16)

    return pl.pallas_call(
        body,
        in_specs=[
            pl.BlockSpec(memory_space=pltpu.SMEM),
            pl.BlockSpec(memory_space=pltpu.VMEM),
            pl.BlockSpec(memory_space=pltpu.VMEM),
        ],
        out_shape=[
            jax.ShapeDtypeStruct((2 * part, hidden), F32),
            jax.ShapeDtypeStruct((2 * part, hidden), BF16),
        ],
        compiler_params=pltpu.CompilerParams(vmem_limit_bytes=48 * 2**20),
        cost_estimate=pl.CostEstimate(
            flops=4 * part * images * half * width, transcendentals=0, bytes_accessed=5 * 2**20
        ),
        name="weight_grad",
    )(me.reshape(1), packed, deltas)


def swap_space(values):
    size = lax.axis_size("space")
    return lax.ppermute(values, "space", [(k, size - 1 - k) for k in range(size)])


def swap_images(values, distance):
    return lax.ppermute(values, "dp", [(k, k ^ distance) for k in range(lax.axis_size("dp"))])


def on_device(feature_map, proposals, hidden_weight, output_weight, upstream):
    images = lax.axis_size("dp")
    assert lax.axis_size("space") == 2 and images & (images - 1) == 0
    own_map = feature_map[0]
    own_height, map_width, channels = own_map.shape
    rois = proposals.shape[1]
    side = lax.axis_index("space")
    me = lax.axis_index("dp").astype(jnp.int32)
    map_own = own_map.reshape(own_height * map_width, channels)
    map_other = swap_space(map_own)
    out_other = swap_space(output_weight)

    corners = jnp.roll(proposals[0], side * (rois // 2), axis=0)
    incoming = jnp.roll(upstream[0], side * (rois // 2), axis=0)

    cell = jnp.arange(2 * own_height * map_width, dtype=jnp.int32)
    row_in_order = cell // map_width
    grid_y = ((row_in_order + side * own_height) % (2 * own_height)).astype(F32)
    grid_x = (cell % map_width).astype(F32)
    ys = sample_points(corners[:, 0], corners[:, 2])
    xs = sample_points(corners[:, 1], corners[:, 3])
    lanes = lambda pts: [p[:, :, None] for p in pts]
    rows = lambda pts: [p[:, None, :] for p in pts]
    row_tab = tent(lanes(ys), grid_y[None, None, :]).astype(BF16)
    col_tab = tent(lanes(xs), grid_x[None, None, :]).astype(BF16)
    row_tab_t = tent(rows(ys), grid_y[None, :, None]).astype(BF16)
    col_tab_t = tent(rows(xs), grid_x[None, :, None]).astype(BF16)

    pre_hidden, packed = crop_forward(row_tab, col_tab, map_own, map_other, hidden_weight, images)
    pre_other = swap_space(pre_hidden.astype(BF16))
    received = lax.all_to_all(packed, "dp", 0, 0, tiled=True)
    delta, mine, second = head(pre_hidden, pre_other, output_weight, out_other, incoming)

    bits = images.bit_length() - 1
    gathered = mine[None]
    place = [0]
    for distance in [1 << b for b in range(bits - 1, -1, -1)]:
        gathered = jnp.concatenate([gathered, swap_images(gathered, distance)], axis=0)
        place = place + [p ^ distance for p in place]
    order = {m: k for k, m in enumerate(place)}

    crops, grad_other = crop_backward_other(row_tab_t, col_tab_t, delta, hidden_weight)
    grad_received = swap_space(grad_other)
    grad_own = crop_backward_own(row_tab_t, col_tab_t, crops)
    map_grad = (grad_own + grad_received.astype(F32)).reshape(own_height, map_width, channels)

    for distance in [1 << b for b in range(bits)]:
        rounded = second.astype(BF16)
        second = rounded.astype(F32) + swap_images(rounded, distance).astype(F32)

    first_own, first_other = weight_grad(received, gathered, order, me)
    first_total = first_own + swap_space(first_other).astype(F32)
    return (first_total, second, map_grad[None])


def solution(mesh):
    placed = (
        P("dp", "space", None, None),
        P("dp", None, None),
        P(None, "space"),
        P("space", None),
        P("dp", None, None),
    )
    return jax.shard_map(
        on_device,
        mesh=mesh,
        in_specs=placed,
        out_specs=(P("dp", "space"), P("space", None), P("dp", "space", None, None)),
        check_vma=False,
    )
```

time: 363 us -> 135 us (0.37)
  waiting for transfers between devices: 175 us -> 40.8 us
  matrix products: 81.6 us -> 0 us
  local copies, waits for them, and re-layouts: 58.4 us -> 4.65 us
  Pallas kernels: 0 us -> 45.4 us
  blocking collectives: 16.2 us -> 0 us
  starting transfers between devices: 6.13 us -> 21.6 us
  between operations: 14 us -> 0.81 us
  other arithmetic: 10.1 us -> 20.8 us
    all_gather x2 -> x0, waiting for transfers between devices: 94.8 us -> none  [the longest x1 50.5 us: on_device(): delta_rows = lax.all_gather(hidden_delta, 'dp', axis=0, tiled=True)]
    dot_general x22 -> x0, matrix products: 81.6 us -> none  [the longest x4 29.9 us: per_block(): jnp.einsum('riy,rjyc->rijc', row_part, across, precision=lax.Precision.HI...]
    psum x2 -> x0, waiting for transfers between devices: 56.8 us -> none  [the longest x1 33.9 us: on_device(): second_total = lax.psum(step_second, 'dp')]
    pallas_call x0 -> x5, Pallas kernels: none -> 45.4 us  [the longest x1 20.4 us: crop_forward(): pl.pallas_call(body, grid=(POOL,), in_specs=[pl.BlockSpec((1, rois, cells...]
    ppermute x0 -> x13, waiting for transfers between devices: none -> 40.8 us  [the longest x8 34 us: swap_images(): lax.ppermute(values, 'dp', [(k, k ^ distance) for k in range(lax.axis_siz...]
    convert_element_type x6 -> x0, local copies, waits for them, and re-layouts: 27.3 us -> none  [the longest x4 26.3 us: on_device(): pooled = crop_rows(whole_map, full_weight, col_weight).astype(jnp.bfloat16)]
    reduce_scatter x1 -> x0, waiting for transfers between devices: 22.2 us -> none  [on_device(): lax.psum_scatter(partial_grad.astype(jnp.bfloat16), 'space', scatter_dime...]
    all_gather x1 -> x0, blocking collectives: 16.2 us -> none  [on_device(): whole_map = lax.all_gather(own_map, 'space', axis=0, tiled=True)]
  transfers between devices with their start and end apart: 6 -> 14, of which waited for: 5 -> 7; matrix products, arithmetic and copies ran while one was open for 23% -> 16% of each run, Pallas kernels for 0% -> 34%
where the time goes in v1:
time: 135 us; the launch traced here: 134 us
  Pallas kernels  45.4 us (34%)
  waiting for transfers between devices  40.8 us (30%)
  starting transfers between devices  21.6 us (16%)
  other arithmetic  20.8 us (15%)
  local copies, waits for them, and re-layouts  4.65 us (3%)
    ppermute x8, waiting for transfers between devices, swap_images(): lax.ppermute(values, 'dp', [(k, k ^ distance) for k in range(lax.axis_siz...  34 us
    pallas_call x1, Pallas kernels, crop_forward(): pl.pallas_call(body, grid=(POOL,), in_specs=[pl.BlockSpec((1, rois, cells...  20.4 us
    pallas_call x1, Pallas kernels, crop_backward_other(): pl.pallas_call(body, grid=(POOL,), in_specs=[pl.BlockSpec((1, half_cells,...  12 us
    pallas_call x1, Pallas kernels, crop_backward_own(): pl.pallas_call(body, grid=(POOL,), in_specs=[pl.BlockSpec((1, half_cells,...  9.55 us
    ppermute x8, starting transfers between devices, swap_images(): lax.ppermute(values, 'dp', [(k, k ^ distance) for k in range(lax.axis_siz...  8.28 us
    convert_element_type x1, other arithmetic, on_device(): col_tab = tent(lanes(xs), grid_x[None, None, :]).astype(BF16)  6.93 us
    convert_element_type x1, other arithmetic, on_device(): col_tab_t = tent(rows(xs), grid_x[None, :, None]).astype(BF16)  6.85 us
    ppermute x5, waiting for transfers between devices, swap_space(): lax.ppermute(values, 'space', [(k, size - 1 - k) for k in range(size)])  6.78 us
  transfers between devices with their start and end apart: 14, of which 7 were waited for; matrix products, arithmetic and copies ran while one was open for 16% of the time, Pallas kernels for 34%

profile of v1, /device:TPU:0, one launch (start us, length us, event | category | flops | bytes accessed | tf_op | source)
XLA Modules:
  0.0 134.0 jit_solution(11624719057305881968)
XLA Ops:
  0.6 1.1 reshape_squeeze.3.own_ref
  1.8 0.0 copy-start.3
  1.8 3.0 %collective-permute-start = (bf16[1008,256]{1,0:T(8,128)(2,1)S(1)}, bf16[1008,256]{1,0:T(8,128)(2,1)S(1)}, u32[]{:S(2)}, u32[]{:S(2)}) collective-permute-start(bf16[1008,256]{1,0:T(8,128)(2,1)S(1)} %reshape_squeeze.3.own_ref), channel_id=1, source_target_pairs={{0,1},{1,0},{2,3},{3,2},{4,5},{5,4},{6,7},{7,6},{8,9},{9,8},{10,11... | collective-permute-start | bytes 1548296 | tf_op jit(solution)/shard_map/ppermute | solution.py:316
  4.8 0.1 collective-permute-start.2
  4.9 0.8 fusion.13
  5.7 0.1 add_add_fusion.3
  5.8 6.9 %multiply_convert_fusion = (bf16[7,128,2016]{2,1,0:T(8,128)(2,1)}, bf16[7,128,2016]{2,1,0:T(8,128)(2,1)}) fusion(f32[7,128]{1,0:T(8,128)S(1)} %get-tuple-element.35, f32[2016]{0:T(1024)S(1)} %fusion.11, f32[7,128]{1,0:T(8,128)S(1)} %get-tuple-element.36, f32[7,128]{1,0:T(8,128)S(1)} %get-tuple-element.34, f32[2016]{0:T(1024)S(1)} %fusion.10, ...), kind=kLoop, calls=%fused_computation | loop fusion | flops 39739392 | bytes 7255808 | tf_op jit(solution)/shard_map/convert_element_type | solution.py:347
  12.7 0.7 fusion.eye_ref
  13.4 4.0 %collective-permute-done.other_ref = bf16[1008,256]{1,0:T(8,128)(2,1)S(1)} collective-permute-done((bf16[1008,256]{1,0:T(8,128)(2,1)S(1)}, bf16[1008,256]{1,0:T(8,128)(2,1)S(1)}, u32[]{:S(2)}, u32[]{:S(2)}) %collective-permute-start) | collective-permute-done | bytes 516128 | tf_op jit(solution)/shard_map/ppermute | solution.py:316
  17.4 0.0 copy-start.5
  17.4 0.0 copy-done.3
  17.4 0.8 copy-done.5
  18.2 20.4 %crop_forward.1 = (f32[128,256]{1,0:T(8,128)}, bf16[16,392,128]{2,1,0:T(8,128)(2,1)}) custom-call(bf16[7,128,2016]{2,1,0:T(8,128)(2,1)} %get-tuple-element.38.row_ref, bf16[7,128,2016]{2,1,0:T(8,128)(2,1)} %get-tuple-element.37.col_ref, bf16[1008,256]{1,0:T(8,128)(2,1)} %copy-done.3, bf16[1008,256]{1,0:T(8,128)(2,1)} %copy-done.5, ...), custom_call_target="tpu_custom_call" | custom-call | flops 6473908224 | bytes 20971520 | tf_op jit(solution)/shard_map/crop_forward/pallas_call | solution.py:106
  38.6 0.0 copy-start
  38.6 0.0 copy-start.4
  38.6 0.0 copy-start.2
  38.6 6.6 %all-to-all-start = ((bf16[16,392,128]{2,1,0:T(8,128)(2,1)}), bf16[16,392,128]{2,1,0:T(8,128)(2,1)S(1)}, u32[]{:S(2)}, u32[]{:S(2)}) async-start(bf16[16,392,128]{2,1,0:T(8,128)(2,1)} %get-tuple-element.12), calls=%async_computation | async-start | bytes 3211264 | tf_op jit(solution)/shard_map/all_to_all | solution.py:353
  45.2 6.8 %multiply_convert_fusion.2 = (bf16[7,2016,128]{2,1,0:T(8,128)(2,1)}, bf16[7,2016,128]{2,1,0:T(8,128)(2,1)}) fusion(f32[7,128]{1,0:T(8,128)S(1)} %get-tuple-element.35, f32[2016]{0:T(1024)S(1)} %fusion.11, f32[7,128]{1,0:T(8,128)S(1)} %get-tuple-element.36, f32[7,128]{1,0:T(8,128)S(1)} %get-tuple-element.34, f32[2016]{0:T(1024)S(1)} %fusion.10, ...), kind=kLoop, calls=%fused_computation.2 | loop fusion | flops 39739392 | bytes 7255808 | tf_op jit(solution)/shard_map/convert_element_type | solution.py:349
  52.1 0.0 copy-done
  52.1 1.6 %collective-permute-start.1 = (bf16[128,256]{1,0:T(8,128)(2,1)S(1)}, bf16[128,256]{1,0:T(8,128)(2,1)S(1)}, u32[]{:S(2)}, u32[]{:S(2)}) collective-permute-start(bf16[128,256]{1,0:T(8,128)(2,1)S(1)} %convert_element_type.153), channel_id=1, source_target_pairs={{0,1},{1,0},{2,3},{3,2},{4,5},{5,4},{6,7},{7,6},{8,9},{9,8},{10,11... | collective-permute-start | bytes 196616 | tf_op jit(solution)/shard_map/ppermute | solution.py:316
  53.6 0.0 copy-done.4
  53.6 0.1 fusion.1.up_ref
  53.7 0.0 collective-permute-done.2.wother_ref
  53.8 2.8 %collective-permute-done.1.recv_ref = bf16[128,256]{1,0:T(8,128)(2,1)S(1)} collective-permute-done((bf16[128,256]{1,0:T(8,128)(2,1)S(1)}, bf16[128,256]{1,0:T(8,128)(2,1)S(1)}, u32[]{:S(2)}, u32[]{:S(2)}) %collective-permute-start.1) | collective-permute-done | bytes 65568 | tf_op jit(solution)/shard_map/ppermute | solution.py:316
  56.5 0.0 copy-done.2
  56.5 0.8 head.1
  57.3 0.0 copy-start.1
  57.3 0.6 copy-done.1
  58.0 2.7 %collective-permute-start.3 = (bf16[1,64,512]{2,1,0:T(8,128)(2,1)S(1)}, bf16[1,64,512]{2,1,0:T(8,128)(2,1)S(1)}, u32[]{:S(2)}, u32[]{:S(2)}) collective-permute-start(bf16[1,64,512]{2,1,0:T(8,128)(2,1)S(1)} %bitcast.13), channel_id=1, source_target_pairs={{0,16},{2,18},{4,20},{6,22},{8,24},{10,26},{12,28},{14,30},{16,0},... | collective-permute-start | bytes 196616 | tf_op jit(solution)/shard_map/ppermute | solution.py:320
  60.7 0.1 collective-permute-start.8
  60.8 12.0 %crop_backward_other.1 = (bf16[6272,256]{1,0:T(8,128)(2,1)}, bf16[1008,256]{1,0:T(8,128)(2,1)}) custom-call(bf16[7,2016,128]{2,1,0:T(8,128)(2,1)} %get-tuple-element.40.row_ref, bf16[7,2016,128]{2,1,0:T(8,128)(2,1)} %get-tuple-element.39.col_ref, bf16[128,256]{1,0:T(8,128)(2,1)} %copy-done.1, bf16[12544,256]{1,0:T(8,128)(2,1)} %weight_ref.3), custom_call_target="tpu_custom_call" | custom-call | flops 3236954112 | bytes 14680064 | tf_op jit(solution)/shard_map/crop_backward_other/pallas_call | solution.py:199
  72.8 13.7 %collective-permute-done.3 = bf16[1,64,512]{2,1,0:T(8,128)(2,1)S(1)} collective-permute-done((bf16[1,64,512]{2,1,0:T(8,128)(2,1)S(1)}, bf16[1,64,512]{2,1,0:T(8,128)(2,1)S(1)}, u32[]{:S(2)}, u32[]{:S(2)}) %collective-permute-start.3) | collective-permute-done | bytes 65568 | tf_op jit(solution)/shard_map/ppermute | solution.py:320
  86.5 0.1 collective-permute-start.4
  86.6 9.5 %crop_backward_own.1 = f32[1008,256]{1,0:T(8,128)} custom-call(bf16[7,2016,128]{2,1,0:T(8,128)(2,1)} %get-tuple-element.40.row_ref, bf16[7,2016,128]{2,1,0:T(8,128)(2,1)} %get-tuple-element.39.col_ref, bf16[6272,256]{1,0:T(8,128)(2,1)} %get-tuple-element.19.crop_ref), custom_call_target="tpu_custom_call" | custom-call | flops 3236954112 | bytes 9437184 | tf_op jit(solution)/shard_map/crop_backward_own/pallas_call | solution.py:248
  96.2 1.5 %collective-permute-start.12 = (bf16[1008,256]{1,0:T(8,128)(2,1)}, bf16[1008,256]{1,0:T(8,128)(2,1)}, u32[]{:S(2)}, u32[]{:S(2)}) collective-permute-start(bf16[1008,256]{1,0:T(8,128)(2,1)} %get-tuple-element.20), channel_id=1, source_target_pairs={{0,1},{1,0},{2,3},{3,2},{4,5},{5,4},{6,7},{7,6},{8,9},{9,8},{10,11... | collective-permute-start | bytes 1548296 | tf_op jit(solution)/shard_map/ppermute | solution.py:316
  97.6 0.0 collective-permute-done.4
  97.7 1.6 %collective-permute-start.5 = (bf16[4,64,512]{2,1,0:T(8,128)(2,1)S(1)}, bf16[4,64,512]{2,1,0:T(8,128)(2,1)S(1)}, u32[]{:S(2)}, u32[]{:S(2)}) collective-permute-start(bf16[4,64,512]{2,1,0:T(8,128)(2,1)S(1)} %pad_maximum_fusion.1), channel_id=1, source_target_pairs={{0,4},{2,6},{4,0},{6,2},{8,12},{10,14},{12,8},{14,10},{16,20},{18,... | collective-permute-start | bytes 786440 | tf_op jit(solution)/shard_map/ppermute | solution.py:320
  99.3 0.0 collective-permute-done.8
  99.3 0.1 add_convert_fusion.2
  99.3 0.6 collective-permute-start.9
  99.9 7.0 %collective-permute-done.5 = bf16[4,64,512]{2,1,0:T(8,128)(2,1)S(1)} collective-permute-done((bf16[4,64,512]{2,1,0:T(8,128)(2,1)S(1)}, bf16[4,64,512]{2,1,0:T(8,128)(2,1)S(1)}, u32[]{:S(2)}, u32[]{:S(2)}) %collective-permute-start.5) | collective-permute-done | bytes 262176 | tf_op jit(solution)/shard_map/ppermute | solution.py:320
  106.9 0.1 pad_maximum_fusion
  107.0 0.1 collective-permute-start.6
  107.1 3.8 %collective-permute-done.9 = bf16[256,512]{1,0:T(8,128)(2,1)S(1)} collective-permute-done((bf16[256,512]{1,0:T(8,128)(2,1)S(1)}, bf16[256,512]{1,0:T(8,128)(2,1)S(1)}, u32[]{:S(2)}, u32[]{:S(2)}) %collective-permute-start.9) | collective-permute-done | bytes 262176 | tf_op jit(solution)/shard_map/ppermute | solution.py:320
  110.8 0.1 add_convert_fusion.1
  110.9 1.8 %collective-permute-start.10 = (bf16[256,512]{1,0:T(8,128)(2,1)S(1)}, bf16[256,512]{1,0:T(8,128)(2,1)S(1)}, u32[]{:S(2)}, u32[]{:S(2)}) collective-permute-start(bf16[256,512]{1,0:T(8,128)(2,1)S(1)} %add_convert_fusion.1), channel_id=1, source_target_pairs={{0,8},{2,10},{4,12},{6,14},{8,0},{10,2},{12,4},{14,6},{16,24},{18,... | collective-permute-start | bytes 786440 | tf_op jit(solution)/shard_map/ppermute | solution.py:320
  112.7 4.9 %collective-permute-done.10 = bf16[256,512]{1,0:T(8,128)(2,1)S(1)} collective-permute-done((bf16[256,512]{1,0:T(8,128)(2,1)S(1)}, bf16[256,512]{1,0:T(8,128)(2,1)S(1)}, u32[]{:S(2)}, u32[]{:S(2)}) %collective-permute-start.10) | collective-permute-done | bytes 262176 | tf_op jit(solution)/shard_map/ppermute | solution.py:320
  117.7 0.8 add_convert_fusion
  118.5 1.4 %collective-permute-start.11 = (bf16[256,512]{1,0:T(8,128)(2,1)}, bf16[256,512]{1,0:T(8,128)(2,1)}, u32[]{:S(2)}, u32[]{:S(2)}) collective-permute-start(bf16[256,512]{1,0:T(8,128)(2,1)} %add_convert_fusion), channel_id=1, source_target_pairs={{0,16},{2,18},{4,20},{6,22},{8,24},{10,26},{12,28},{14,30},{16,0},... | collective-permute-start | bytes 786440 | tf_op jit(solution)/shard_map/ppermute | solution.py:320
  119.9 0.0 collective-permute-done.6
  119.9 0.0 all-to-all-done.packed_ref
  119.9 2.7 %weight_grad.1 = (f32[784,256]{1,0:T(8,128)S(1)}, bf16[784,256]{1,0:T(8,128)(2,1)}) custom-call(s32[1]{0:T(128)} %bitcast.me_ref, bf16[16,392,128]{2,1,0:T(8,128)(2,1)S(1)} %all-to-all-done.packed_ref, bf16[16,64,512]{2,1,0:T(8,128)(2,1)S(1)} %constant_dynamic-update-slice_fusion.delta_ref), custom_call_target="tpu_custom_call" | custom-call | flops 822083584 | bytes 5242880 | tf_op jit(solution)/shard_map/weight_grad/pallas_call | solution.py:295
  122.6 0.5 collective-permute-start.7
  123.1 0.0 collective-permute-done.12
  123.1 1.5 %convert_add_fusion = f32[1008,256]{1,0:T(8,128)S(1)} fusion(f32[1008,256]{1,0:T(8,128)} %crop_backward_own.1, bf16[1008,256]{1,0:T(8,128)(2,1)} %collective-permute-done.12), kind=kLoop, calls=%fused_computation.4 | loop fusion | flops 516096 | bytes 2580480 | tf_op jit(solution)/shard_map/add | solution.py:367
  124.6 2.0 %broadcast_in_dim_reshape.4 = f32[1,12,84,256]{3,0,2,1:T(1,128)} reshape(f32[1008,256]{1,0:T(8,128)S(1)} %convert_add_fusion) | data formatting | bytes 2064384 | tf_op jit(solution)/shard_map/broadcast_in_dim;reshape | solution.py:375
  126.6 4.5 %collective-permute-done.11 = bf16[256,512]{1,0:T(8,128)(2,1)} collective-permute-done((bf16[256,512]{1,0:T(8,128)(2,1)}, bf16[256,512]{1,0:T(8,128)(2,1)}, u32[]{:S(2)}, u32[]{:S(2)}) %collective-permute-start.11) | collective-permute-done | bytes 262176 | tf_op jit(solution)/shard_map/ppermute | solution.py:320
  131.1 1.9 %convert_add_fusion.2 = f32[256,512]{1,0:T(8,128)} fusion(bf16[256,512]{1,0:T(8,128)(2,1)} %collective-permute-done.11, bf16[256,512]{1,0:T(8,128)(2,1)} %add_convert_fusion), kind=kLoop, calls=%fused_computation.7 | loop fusion | flops 393216 | bytes 1048576 | tf_op jit(solution)/shard_map/add | solution.py:371
  133.0 0.0 collective-permute-done.7
  133.0 1.0 convert_add_fusion.1
  (15 shorter events, 0.2 us)
Async XLA Ops:
  1.8 15.6 %copy-start.3 = (bf16[1008,256]{1,0:T(8,128)(2,1)}, bf16[1008,256]{1,0:T(8,128)(2,1)S(1)}, u32[]{:S(2)}) copy-start(bf16[1008,256]{1,0:T(8,128)(2,1)S(1)} %reshape_squeeze.3.own_ref) | copy-start | bytes 1548292
  1.8 15.6 %collective-permute-start = (bf16[1008,256]{1,0:T(8,128)(2,1)S(1)}, bf16[1008,256]{1,0:T(8,128)(2,1)S(1)}, u32[]{:S(2)}, u32[]{:S(2)}) collective-permute-start(bf16[1008,256]{1,0:T(8,128)(2,1)S(1)} %reshape_squeeze.3.own_ref), channel_id=1, source_target_pairs={{0,1},{1,0},{2,3},{3,2},{4,5},{5,4},{6,7},{7,6},{8,9},{9,8},{10,11... | collective-permute-start | bytes 1548296 | tf_op jit(solution)/shard_map/ppermute | solution.py:316
  4.8 48.9 %collective-permute-start.2 = (bf16[256,512]{1,0:T(8,128)(2,1)}, bf16[256,512]{1,0:T(8,128)(2,1)S(1)}, u32[]{:S(2)}, u32[]{:S(2)}) collective-permute-start(bf16[256,512]{1,0:T(8,128)(2,1)} %wown_ref.1), channel_id=1, source_target_pairs={{0,1},{1,0},{2,3},{3,2},{4,5},{5,4},{6,7},{7,6},{8,9},{9,8},{10,11... | collective-permute-start | bytes 786440 | tf_op jit(solution)/shard_map/ppermute | solution.py:316
  17.4 0.8 copy-start.5
  38.6 13.5 %copy-start = (f32[128,256]{1,0:T(8,128)S(1)}, f32[128,256]{1,0:T(8,128)}, u32[]{:S(2)}) copy-start(f32[128,256]{1,0:T(8,128)} %get-tuple-element.13.own_ref) | copy-start | bytes 393220
  38.6 15.1 %copy-start.4 = (bf16[1,128,512]{2,1,0:T(8,128)(2,1)S(1)}, bf16[1,128,512]{2,1,0:T(8,128)(2,1)}, u32[]{:S(2)}) copy-start(bf16[1,128,512]{2,1,0:T(8,128)(2,1)} %param.9) | copy-start | bytes 393220
  38.6 18.0 %copy-start.2 = (bf16[256,512]{1,0:T(8,128)(2,1)S(1)}, bf16[256,512]{1,0:T(8,128)(2,1)}, u32[]{:S(2)}) copy-start(bf16[256,512]{1,0:T(8,128)(2,1)} %wown_ref.1) | copy-start | bytes 786436
  38.6 81.4 %all-to-all-start = ((bf16[16,392,128]{2,1,0:T(8,128)(2,1)}), bf16[16,392,128]{2,1,0:T(8,128)(2,1)S(1)}, u32[]{:S(2)}, u32[]{:S(2)}) async-start(bf16[16,392,128]{2,1,0:T(8,128)(2,1)} %get-tuple-element.12), calls=%async_computation | async-start | bytes 3211264 | tf_op jit(solution)/shard_map/all_to_all | solution.py:353
  52.1 4.5 %collective-permute-start.1 = (bf16[128,256]{1,0:T(8,128)(2,1)S(1)}, bf16[128,256]{1,0:T(8,128)(2,1)S(1)}, u32[]{:S(2)}, u32[]{:S(2)}) collective-permute-start(bf16[128,256]{1,0:T(8,128)(2,1)S(1)} %convert_element_type.153), channel_id=1, source_target_pairs={{0,1},{1,0},{2,3},{3,2},{4,5},{5,4},{6,7},{7,6},{8,9},{9,8},{10,11... | collective-permute-start | bytes 196616 | tf_op jit(solution)/shard_map/ppermute | solution.py:316
  57.3 0.6 copy-start.1
  58.0 28.6 %collective-permute-start.3 = (bf16[1,64,512]{2,1,0:T(8,128)(2,1)S(1)}, bf16[1,64,512]{2,1,0:T(8,128)(2,1)S(1)}, u32[]{:S(2)}, u32[]{:S(2)}) collective-permute-start(bf16[1,64,512]{2,1,0:T(8,128)(2,1)S(1)} %bitcast.13), channel_id=1, source_target_pairs={{0,16},{2,18},{4,20},{6,22},{8,24},{10,26},{12,28},{14,30},{16,0},... | collective-permute-start | bytes 196616 | tf_op jit(solution)/shard_map/ppermute | solution.py:320
  60.7 38.6 %collective-permute-start.8 = (bf16[256,512]{1,0:T(8,128)(2,1)S(1)}, bf16[256,512]{1,0:T(8,128)(2,1)S(1)}, u32[]{:S(2)}, u32[]{:S(2)}) collective-permute-start(bf16[256,512]{1,0:T(8,128)(2,1)S(1)} %convert_element_type.155), channel_id=1, source_target_pairs={{0,2},{2,0},{4,6},{6,4},{8,10},{10,8},{12,14},{14,12},{16,18},{18,... | collective-permute-start | bytes 786440 | tf_op jit(solution)/shard_map/ppermute | solution.py:320
  86.5 11.1 %collective-permute-start.4 = (bf16[2,64,512]{2,1,0:T(8,128)(2,1)S(1)}, bf16[2,64,512]{2,1,0:T(8,128)(2,1)S(1)}, u32[]{:S(2)}, u32[]{:S(2)}) collective-permute-start(bf16[2,64,512]{2,1,0:T(8,128)(2,1)S(1)} %pad_maximum_fusion.2), channel_id=1, source_target_pairs={{0,8},{2,10},{4,12},{6,14},{8,0},{10,2},{12,4},{14,6},{16,24},{18,... | collective-permute-start | bytes 393224 | tf_op jit(solution)/shard_map/ppermute | solution.py:320
  96.2 27.0 %collective-permute-start.12 = (bf16[1008,256]{1,0:T(8,128)(2,1)}, bf16[1008,256]{1,0:T(8,128)(2,1)}, u32[]{:S(2)}, u32[]{:S(2)}) collective-permute-start(bf16[1008,256]{1,0:T(8,128)(2,1)} %get-tuple-element.20), channel_id=1, source_target_pairs={{0,1},{1,0},{2,3},{3,2},{4,5},{5,4},{6,7},{7,6},{8,9},{9,8},{10,11... | collective-permute-start | bytes 1548296 | tf_op jit(solution)/shard_map/ppermute | solution.py:316
  97.7 9.2 %collective-permute-start.5 = (bf16[4,64,512]{2,1,0:T(8,128)(2,1)S(1)}, bf16[4,64,512]{2,1,0:T(8,128)(2,1)S(1)}, u32[]{:S(2)}, u32[]{:S(2)}) collective-permute-start(bf16[4,64,512]{2,1,0:T(8,128)(2,1)S(1)} %pad_maximum_fusion.1), channel_id=1, source_target_pairs={{0,4},{2,6},{4,0},{6,2},{8,12},{10,14},{12,8},{14,10},{16,20},{18,... | collective-permute-start | bytes 786440 | tf_op jit(solution)/shard_map/ppermute | solution.py:320
  99.3 11.5 %collective-permute-start.9 = (bf16[256,512]{1,0:T(8,128)(2,1)S(1)}, bf16[256,512]{1,0:T(8,128)(2,1)S(1)}, u32[]{:S(2)}, u32[]{:S(2)}) collective-permute-start(bf16[256,512]{1,0:T(8,128)(2,1)S(1)} %add_convert_fusion.2), channel_id=1, source_target_pairs={{0,4},{2,6},{4,0},{6,2},{8,12},{10,14},{12,8},{14,10},{16,20},{18,... | collective-permute-start | bytes 786440 | tf_op jit(solution)/shard_map/ppermute | solution.py:320
  107.0 12.9 %collective-permute-start.6 = (bf16[8,64,512]{2,1,0:T(8,128)(2,1)S(1)}, bf16[8,64,512]{2,1,0:T(8,128)(2,1)S(1)}, u32[]{:S(2)}, u32[]{:S(2)}) collective-permute-start(bf16[8,64,512]{2,1,0:T(8,128)(2,1)S(1)} %pad_maximum_fusion), channel_id=1, source_target_pairs={{0,2},{2,0},{4,6},{6,4},{8,10},{10,8},{12,14},{14,12},{16,18},{18,... | collective-permute-start | bytes 1572872 | tf_op jit(solution)/shard_map/ppermute | solution.py:320
  110.9 6.8 %collective-permute-start.10 = (bf16[256,512]{1,0:T(8,128)(2,1)S(1)}, bf16[256,512]{1,0:T(8,128)(2,1)S(1)}, u32[]{:S(2)}, u32[]{:S(2)}) collective-permute-start(bf16[256,512]{1,0:T(8,128)(2,1)S(1)} %add_convert_fusion.1), channel_id=1, source_target_pairs={{0,8},{2,10},{4,12},{6,14},{8,0},{10,2},{12,4},{14,6},{16,24},{18,... | collective-permute-start | bytes 786440 | tf_op jit(solution)/shard_map/ppermute | solution.py:320
  118.5 12.7 %collective-permute-start.11 = (bf16[256,512]{1,0:T(8,128)(2,1)}, bf16[256,512]{1,0:T(8,128)(2,1)}, u32[]{:S(2)}, u32[]{:S(2)}) collective-permute-start(bf16[256,512]{1,0:T(8,128)(2,1)} %add_convert_fusion), channel_id=1, source_target_pairs={{0,16},{2,18},{4,20},{6,22},{8,24},{10,26},{12,28},{14,30},{16,0},... | collective-permute-start | bytes 786440 | tf_op jit(solution)/shard_map/ppermute | solution.py:320
  122.6 10.4 %collective-permute-start.7 = (bf16[784,256]{1,0:T(8,128)(2,1)}, bf16[784,256]{1,0:T(8,128)(2,1)S(1)}, u32[]{:S(2)}, u32[]{:S(2)}) collective-permute-start(bf16[784,256]{1,0:T(8,128)(2,1)} %get-tuple-element.16), channel_id=1, source_target_pairs={{0,1},{1,0},{2,3},{3,2},{4,5},{5,4},{6,7},{7,6},{8,9},{9,8},{10,11... | collective-permute-start | bytes 1204232 | tf_op jit(solution)/shard_map/ppermute | solution.py:316

commit v2 on v0

v2 whole, which is shorter than its diff:
```python
import jax
import jax.numpy as jnp
from jax import lax
from jax.experimental import pallas as pl
from jax.experimental.pallas import tpu as pltpu
from jax.sharding import PartitionSpec as P


POOL = 7
BINS = POOL * POOL
F32 = jnp.float32
BF16 = jnp.bfloat16


def activate(values):
    return jax.nn.gelu(values, approximate=True)


def gelu_grad(values, incoming):
    return jax.vjp(activate, values)[1](incoming)[0]


def sample_points(low_edge, high_edge):
    edge_start = low_edge.astype(F32)
    bin_size = (high_edge - low_edge).astype(F32) / POOL
    bin_index = jnp.arange(POOL).astype(F32)
    return [
        edge_start[None, :] + (bin_index[:, None] + offset) * bin_size[None, :] - 0.5
        for offset in (0.25, 0.75)
    ]


def tent(first, second, grid):
    return 0.5 * (
        jnp.maximum(0.0, 1.0 - jnp.abs(first - grid))
        + jnp.maximum(0.0, 1.0 - jnp.abs(second - grid))
    )


def dot(a, b, dims=((1,), (0,))):
    return lax.dot_general(a, b, (dims, ((), ())), preferred_element_type=F32)


LIMIT = 13
TAPS = 128


def kernel(body, out_shape, scratch=(), flops=10**9, limit=LIMIT, smem_first=False, anywhere=(), hbm_out=False):
    def call(*args):
        specs = [pl.BlockSpec(memory_space=pltpu.VMEM) for _ in args]
        if smem_first:
            specs[0] = pl.BlockSpec(memory_space=pltpu.SMEM)
        args = list(args)
        for k in anywhere:
            args[k] = pltpu.with_memory_space_constraint(args[k], pltpu.HBM)
            specs[k] = pl.BlockSpec(memory_space=pltpu.HBM)
        out_space = pltpu.HBM if hbm_out else pltpu.VMEM
        return pl.pallas_call(
            body,
            in_specs=specs,
            out_specs=jax.tree.map(lambda _: pl.BlockSpec(memory_space=out_space), out_shape),
            out_shape=out_shape,
            scratch_shapes=scratch,
            compiler_params=pltpu.CompilerParams(vmem_limit_bytes=limit * 2**20),
            cost_estimate=pl.CostEstimate(
                flops=int(flops), transcendentals=0, bytes_accessed=2**20
            ),
        )(*args)

    return call


def fetch(source, target, sems):
    rows = target.shape[0] // POOL
    copies = []
    for k in range(POOL):
        at = pl.ds(k * rows, rows)
        copies.append(pltpu.make_async_copy(source.at[at], target.at[at], sems.at[k]))
        copies[-1].start()
    return copies


def shaped(dtype, *shape):
    return jax.ShapeDtypeStruct(shape, dtype)


def spread(taps, cells, width, real, transposed=False):
    shape = (cells, 1) if transposed else (1, cells)
    cell = lax.broadcasted_iota(jnp.int32, shape, 0 if transposed else 1).astype(F32)
    row = jnp.floor((cell + 0.5) * (1.0 / width))
    column = jnp.where(cell < real, cell - row * width, -1.0)
    row = jnp.where(cell < real, row, -1.0)
    full = (cells, taps) if transposed else (taps, cells)
    tap = lax.broadcasted_iota(jnp.int32, full, 1 if transposed else 0).astype(F32)
    one = lambda where: jnp.where(tap == where, 1.0, 0.0).astype(BF16)
    return one(column), one(row)


def crop_own(points, map_own, width, real):
    count = points.shape[0]
    rois = count // POOL
    cells, channels = map_own.shape

    def body(pts, map_ref, col_ref, other_ref, part_ref, own_ref, w_a, w_b):
        sx, sy = spread(TAPS, cells, width, real)
        grid = lax.broadcasted_iota(jnp.int32, (count, TAPS), 1).astype(F32)
        weights = [tent(pts[:, k : k + 1], pts[:, k + 1 : k + 2], grid).astype(BF16) for k in (0, 2, 4)]
        col_ref[...] = dot(weights[0], sx).astype(BF16)
        own_ref[...] = dot(weights[1], sy).astype(BF16)
        other_ref[...] = dot(weights[2], sy).astype(BF16)
        for i in range(POOL):
            w2 = (w_a, w_b)[i % 2]
            for j in range(POOL):
                at = slice(j * rois, (j + 1) * rois)
                w2[at, :] = own_ref[i * rois : (i + 1) * rois, :] * col_ref[at, :]
            part_ref[i * count : (i + 1) * count, :] = dot(w2[...], map_ref[...])

    table = shaped(BF16, count, cells)
    return kernel(
        body,
        [table, table, shaped(F32, POOL * count, channels)],
        [pltpu.VMEM((count, cells), BF16)] * 3,
        2 * BINS * rois * cells * channels,
        limit=20,
    )(points, map_own)


def crop_all(col, row, map_other, partial, weight, owners):
    count, cells = col.shape
    rois = count // POOL
    half = rois // 2
    channels = map_other.shape[1]
    hidden = weight.shape[1]
    owned = BINS * channels // owners
    part = owned // 2
    aligned = owned % 16 == 0

    def body(col_ref, row_ref, map_ref, partial_ref, weight_ref, pre_ref, send_ref, pack_ref, w_a, w_b, crops_t):
        ahead = lax.broadcasted_iota(jnp.int32, (channels, channels), 0)
        eye = (ahead == lax.broadcasted_iota(jnp.int32, (channels, channels), 1)).astype(BF16)
        acc = jnp.zeros((rois, hidden), F32)
        for i in range(POOL):
            w2 = (w_a, w_b)[i % 2]
            for j in range(POOL):
                at = slice(j * rois, (j + 1) * rois)
                w2[at, :] = row_ref[i * rois : (i + 1) * rois, :] * col_ref[at, :]
            block = slice(i * count, (i + 1) * count)
            pooled = (partial_ref[block, :] + dot(w2[...], map_ref[...])).astype(BF16)
            for j in range(POOL):
                crop = pooled[j * rois : (j + 1) * rois]
                rows = slice((i * POOL + j) * channels, (i * POOL + j + 1) * channels)
                acc += dot(crop, weight_ref[rows, :])
                twice = jnp.concatenate([crop[:half], crop[:half]], axis=0)
                crops_t[rows, :] = dot(eye, twice, ((1,), (1,)))
        pre_ref[...] = acc
        send_ref[...] = acc.astype(BF16)
        if aligned:
            left = lax.broadcasted_iota(jnp.int32, (part, 2 * half), 1) < half
            for e in range(owners):
                first = crops_t[e * owned : e * owned + part, :]
                second = crops_t[e * owned + part : (e + 1) * owned, :]
                pack_ref[e] = jnp.where(left, first, second).astype(BF16)
        else:
            pack_ref[...] = crops_t[...].astype(BF16)

    pack = (owners, part, 2 * half) if aligned else (BINS * channels, 2 * half)
    pre_hidden, sent, packed = kernel(
        body,
        [shaped(F32, rois, hidden), shaped(BF16, rois, hidden), shaped(BF16, *pack)],
        [pltpu.VMEM((count, cells), BF16)] * 2
        + [pltpu.VMEM((BINS * channels, 2 * half), F32)],
        2 * BINS * rois * cells * channels,
        limit=32,
    )(col, row, map_other, partial, weight)
    if not aligned:
        packed = packed[:, :half].reshape(owners, owned, half)
    return pre_hidden, sent, packed


def head(pre_own, pre_received, out_own, out_other, upstream):
    rois, hidden = pre_own.shape
    outputs = out_own.shape[1]
    half = rois // 2

    def body(own_ref, recv_ref, wown_ref, wother_ref, up_ref, hd_ref, mine_ref, grad_ref):
        pre_a = own_ref[...]
        pre_b = jnp.concatenate([recv_ref[half:], recv_ref[:half]], axis=0).astype(F32)
        hid_a = activate(pre_a).astype(BF16)
        hid_b = activate(pre_b).astype(BF16)
        pre_output = dot(hid_a, wown_ref[...]) + dot(hid_b, wother_ref[...])
        delta = gelu_grad(pre_output, up_ref[...].astype(F32)).astype(BF16)
        grad_ref[...] = dot(hid_a, delta, ((0,), (0,)))
        hd_a = gelu_grad(pre_a, dot(delta, wown_ref[...], ((1,), (1,)))).astype(BF16)
        hd_b = gelu_grad(
            pre_b[:half], dot(delta[:half], wother_ref[...], ((1,), (1,)))
        ).astype(BF16)
        hd_ref[...] = hd_a
        mine_ref[:, :hidden] = hd_a[:half]
        mine_ref[:, hidden:] = hd_b

    return pl.pallas_call(
        body,
        out_shape=[
            jax.ShapeDtypeStruct((rois, hidden), BF16),
            jax.ShapeDtypeStruct((half, 2 * hidden), BF16),
            jax.ShapeDtypeStruct((hidden, outputs), F32),
        ],
        compiler_params=pltpu.CompilerParams(vmem_limit_bytes=8 * 2**20),
        cost_estimate=pl.CostEstimate(flops=2 * 10**9, transcendentals=0, bytes_accessed=2**21),
        name="head",
    )(pre_own, pre_received, out_own, out_other, upstream)


def tables_t(pts, which, cells, width, rows_ref, cols_ref):
    pts = pts[...]
    sx, sy = spread(TAPS, cells, width, cells, transposed=True)
    grid = lax.broadcasted_iota(jnp.int32, (TAPS, pts.shape[1]), 0).astype(F32)
    cols_ref[...] = dot(sx, tent(pts[0:1], pts[1:2], grid).astype(BF16)).astype(BF16)
    rows_ref[...] = dot(sy, tent(pts[which : which + 1], pts[which + 1 : which + 2], grid).astype(BF16)).astype(BF16)


def crop_backward_other(points, delta, weight, cells, width):
    count = points.shape[1]
    rois = count // POOL
    channels = weight.shape[0] // BINS

    def body(pts, delta_ref, weight_hbm, crop_ref, out_ref, w_a, w_b, row_ref, col_ref, acc, weight_ref, sems):
        copies = fetch(weight_hbm, weight_ref, sems)
        tables_t(pts, 4, cells, width, row_ref, col_ref)
        for copy in copies:
            copy.wait()
        for i in range(POOL):
            w2 = (w_a, w_b)[i % 2]
            for j in range(POOL):
                k = i * POOL + j
                at = slice(j * rois, (j + 1) * rois)
                w2[:, at] = row_ref[:, i * rois : (i + 1) * rois] * col_ref[:, at]
                crop_ref[k * rois : (k + 1) * rois, :] = dot(
                    delta_ref[...], weight_ref[k * channels : (k + 1) * channels, :], ((1,), (1,))
                ).astype(BF16)
            part = dot(w2[...], crop_ref[i * count : (i + 1) * count, :])
            if i == 0:
                acc[...] = part
            elif i < POOL - 1:
                acc[...] += part
            else:
                out_ref[...] = (acc[...] + part).astype(BF16)

    return kernel(
        body,
        [shaped(BF16, BINS * rois, channels), shaped(BF16, cells, channels)],
        [pltpu.VMEM((cells, count), BF16)] * 4
        + [pltpu.VMEM((cells, channels), F32), pltpu.VMEM(weight.shape, BF16)]
        + [pltpu.SemaphoreType.DMA((POOL,))],
        2 * BINS * rois * cells * channels,
        limit=28,
        anywhere=(2,),
    )(points, delta, weight)


def crop_backward_own(points, crops, cells, width):
    count = points.shape[1]
    rois = count // POOL
    channels = crops.shape[1]

    def body(pts, crop_hbm, acc, w_a, w_b, row_ref, col_ref, crop_ref, sems):
        copies = fetch(crop_hbm, crop_ref, sems)
        tables_t(pts, 2, cells, width, row_ref, col_ref)
        for copy in copies:
            copy.wait()
        for i in range(POOL):
            w2 = (w_a, w_b)[i % 2]
            for j in range(POOL):
                at = slice(j * rois, (j + 1) * rois)
                w2[:, at] = row_ref[:, i * rois : (i + 1) * rois] * col_ref[:, at]
            part = dot(w2[...], crop_ref[i * count : (i + 1) * count, :])
            if i == 0:
                acc[...] = part
            else:
                acc[...] += part

    return kernel(
        body,
        shaped(F32, cells, channels),
        [pltpu.VMEM((cells, count), BF16)] * 4
        + [pltpu.VMEM(crops.shape, BF16), pltpu.SemaphoreType.DMA((POOL,))],
        2 * BINS * rois * cells * channels,
        limit=28,
        anywhere=(1,),
    )(points, crops)


def add_received(own, received):
    def body(own_ref, recv_ref, out_ref):
        out_ref[...] = own_ref[...] + recv_ref[...].astype(F32)

    return kernel(body, shaped(F32, *own.shape), flops=10**8)(own, received)


def weight_grad(packed, deltas, order, me):
    half, width = deltas[0].shape[1:]
    hidden = width // 2
    images, part, lanes = packed.shape
    if lanes == half:
        place = jnp.array([order[m] for m in range(images)])
        in_order = jnp.concatenate(deltas, axis=0)[place[jnp.arange(images) ^ me]]
        total = jnp.einsum("mpr,mrh->ph", packed, in_order, preferred_element_type=F32)
        return total[:, :hidden], total[:, hidden:].astype(BF16)

    def body(me_ref, packed_ref, *refs):
        sources, refs = refs[: len(deltas)], refs[len(deltas) :]
        own_ref, other_ref, *delta_refs, sems = refs
        copies = [
            pltpu.make_async_copy(source, target, sems.at[k])
            for k, (source, target) in enumerate(zip(sources, delta_refs))
        ]
        for copy in copies:
            copy.start()
        for copy in copies:
            copy.wait()
        blocks = [(ref, k) for ref in delta_refs for k in range(ref.shape[0])]
        left = lax.broadcasted_iota(jnp.int32, (part, lanes), 1) < half
        tops = jnp.zeros((part, width), F32)
        bottoms = jnp.zeros((part, width), F32)
        for m in range(0, images, 2):
            a = packed_ref[me_ref[0] ^ m].astype(F32)
            b = packed_ref[me_ref[0] ^ (m + 1)].astype(F32)
            pair = [blocks[order[k]] for k in (m, m + 1)]
            pair = jnp.concatenate([ref[k] for ref, k in pair], axis=0)
            top = jnp.where(left, a, pltpu.roll(b, half, 1)).astype(BF16)
            bottom = jnp.where(left, pltpu.roll(a, half, 1), b).astype(BF16)
            tops += dot(top, pair)
            bottoms += dot(bottom, pair)
        own_ref[:part] = tops[:, :hidden]
        own_ref[part:] = bottoms[:, :hidden]
        other_ref[:part] = tops[:, hidden:].astype(BF16)
        other_ref[part:] = bottoms[:, hidden:].astype(BF16)

    return kernel(
        body,
        [shaped(F32, 2 * part, hidden), shaped(BF16, 2 * part, hidden)],
        [pltpu.VMEM(v.shape, BF16) for v in deltas] + [pltpu.SemaphoreType.DMA((len(deltas),))],
        flops=4 * part * images * half * width,
        limit=16,
        smem_first=True,
        anywhere=range(2, 2 + len(deltas)),
    )(me.reshape(1), packed, *deltas)


def swap_space(values):
    size = lax.axis_size("space")
    return lax.ppermute(values, "space", [(k, size - 1 - k) for k in range(size)])


def swap_images(values, distance):
    return lax.ppermute(values, "dp", [(k, k ^ distance) for k in range(lax.axis_size("dp"))])


def step(feature_map, proposals, hidden_weight, output_weight, upstream):
    images = lax.axis_size("dp")
    assert lax.axis_size("space") == 2 and images & (images - 1) == 0
    bits = images.bit_length() - 1
    own_map = feature_map[0]
    own_height, map_width, channels = own_map.shape
    rois = proposals.shape[1]
    side = lax.axis_index("space")
    me = lax.axis_index("dp").astype(jnp.int32)
    half_cells = own_height * map_width
    padded = -(-half_cells // 128) * 128
    map_own = jnp.pad(own_map.reshape(half_cells, channels), ((0, padded - half_cells), (0, 0)))
    map_other = swap_space(map_own)
    out_other = swap_space(output_weight)

    corners = jnp.roll(proposals[0], side * (rois // 2), axis=0)
    incoming = jnp.roll(upstream[0], side * (rois // 2), axis=0)

    ys = sample_points(corners[:, 0], corners[:, 2])
    xs = sample_points(corners[:, 1], corners[:, 3])
    first_own = (side * own_height).astype(F32)
    first_other = ((1 - side) * own_height).astype(F32)
    points = jnp.stack(
        [p.reshape(-1) for p in xs + [y - f for f in (first_own, first_other) for y in ys]]
    )

    points = jnp.pad(points, ((0, 2), (0, 0)))
    columns = jnp.pad(points.T, ((0, 0), (0, TAPS - points.shape[0])))
    col, row_other, partial = crop_own(columns, map_own, map_width, half_cells)
    pre_hidden, pre_sent, packed = crop_all(
        col, row_other, map_other, partial, hidden_weight, images
    )
    received = lax.all_to_all(packed, "dp", 0, 0, tiled=True)
    pre_other = swap_space(pre_sent)
    delta, mine, second = head(pre_hidden, pre_other, output_weight, out_other, incoming)

    near = [1 << b for b in range(min(2, bits))]
    far = [m for m in range(0, images, 1 << len(near))]
    place = [0]
    gathered = mine[None]
    pieces = [gathered]
    for m in far[1:]:
        pieces.append(swap_images(gathered, m))
    pieces = [jnp.concatenate(pieces, axis=0)]
    place = list(far)
    for distance in near[::-1]:
        pieces = pieces + [swap_images(piece, distance) for piece in pieces]
        place = place + [p ^ distance for p in place]
    order = {m: k for k, m in enumerate(place)}

    crop_grads, grad_other = crop_backward_other(
        points, delta, hidden_weight, half_cells, map_width
    )
    grad_received = swap_space(grad_other)
    grad_own = crop_backward_own(points, crop_grads, half_cells, map_width)
    map_grad = add_received(grad_own, grad_received)
    map_grad = map_grad.reshape(own_height, map_width, channels)

    for distance in near:
        rows = second.shape[0] // 2
        high = (me // distance) % 2
        kept = lax.dynamic_slice_in_dim(second, high * rows, rows, 0)
        sent = lax.dynamic_slice_in_dim(second, (1 - high) * rows, rows, 0)
        theirs = swap_images(sent.astype(BF16), distance)
        second = kept + theirs.astype(F32)
    rounded = second.astype(BF16)
    parts = [rounded] + [swap_images(rounded, m) for m in far[1:]]
    parts = [p.astype(F32) for p in parts]
    while len(parts) > 1:
        parts = [parts[k] + parts[k + 1] for k in range(0, len(parts), 2)]
    second = parts[0]
    second = second.astype(BF16)
    for distance in near[::-1]:
        high = (me // distance) % 2
        theirs = swap_images(second, distance)
        low_part = jnp.where(high == 0, second, theirs)
        high_part = jnp.where(high == 0, theirs, second)
        second = jnp.concatenate([low_part, high_part], axis=0)
    second = second.astype(F32)

    first_own, first_other = weight_grad(received, pieces, order, me)
    first_received = swap_space(first_other)
    return (first_own + first_received.astype(F32), second, map_grad[None])


def solution(mesh):
    placed = (
        P("dp", "space", None, None),
        P("dp", None, None),
        P(None, "space"),
        P("space", None),
        P("dp", None, None),
    )
    return jax.shard_map(
        step,
        mesh=mesh,
        in_specs=placed,
        out_specs=(P("dp", "space"), P("space", None), P("dp", "space", None, None)),
        check_vma=False,
    )
```

time: 363 us -> 123 us (0.34)
  waiting for transfers between devices: 175 us -> 37.1 us
  matrix products: 81.6 us -> 0 us
  local copies, waits for them, and re-layouts: 58.4 us -> 5.94 us
  Pallas kernels: 0 us -> 45.1 us
  starting transfers between devices: 6.13 us -> 30.1 us
  blocking collectives: 16.2 us -> 0 us
  between operations: 14 us -> 0.97 us
  other arithmetic: 10.1 us -> 3.86 us
    all_gather x2 -> x0, waiting for transfers between devices: 94.8 us -> none  [the longest x1 50.5 us: on_device(): delta_rows = lax.all_gather(hidden_delta, 'dp', axis=0, tiled=True)]
    dot_general x22 -> x0, matrix products: 81.6 us -> none  [the longest x4 29.9 us: per_block(): jnp.einsum('riy,rjyc->rijc', row_part, across, precision=lax.Precision.HI...]
    psum x2 -> x0, waiting for transfers between devices: 56.8 us -> none  [the longest x1 33.9 us: on_device(): second_total = lax.psum(step_second, 'dp')]
    pallas_call x0 -> x7, Pallas kernels: none -> 45.1 us  [the longest x6 44.3 us: call(): pl.pallas_call(body, in_specs=specs, out_specs=jax.tree.map(lambda _: pl....]
    ppermute x0 -> x18, waiting for transfers between devices: none -> 37.1 us  [the longest x13 23.6 us: swap_images(): lax.ppermute(values, 'dp', [(k, k ^ distance) for k in range(lax.axis_siz...]
    convert_element_type x6 -> x2, local copies, waits for them, and re-layouts: 27.3 us -> 0.05 us  [step(): theirs = swap_images(sent.astype(BF16), distance)]
    ppermute x0 -> x18, starting transfers between devices: none -> 23.8 us  [the longest x13 16.6 us: swap_images(): lax.ppermute(values, 'dp', [(k, k ^ distance) for k in range(lax.axis_siz...]
    reduce_scatter x1 -> x0, waiting for transfers between devices: 22.2 us -> none  [on_device(): lax.psum_scatter(partial_grad.astype(jnp.bfloat16), 'space', scatter_dime...]
  transfers between devices with their start and end apart: 6 -> 19, of which waited for: 5 -> 9; matrix products, arithmetic and copies ran while one was open for 23% -> 4% of each run, Pallas kernels for 0% -> 28%
where the time goes in v2:
time: 123 us
  Pallas kernels  45.1 us (37%)
  waiting for transfers between devices  37.1 us (30%)
  starting transfers between devices  30.1 us (24%)
  local copies, waits for them, and re-layouts  5.94 us (5%)
  other arithmetic  3.86 us (3%)
    pallas_call x6, Pallas kernels, call(): pl.pallas_call(body, in_specs=specs, out_specs=jax.tree.map(lambda _: pl....  44.3 us
    ppermute x13, waiting for transfers between devices, swap_images(): lax.ppermute(values, 'dp', [(k, k ^ distance) for k in range(lax.axis_siz...  23.6 us
    ppermute x13, starting transfers between devices, swap_images(): lax.ppermute(values, 'dp', [(k, k ^ distance) for k in range(lax.axis_siz...  16.6 us
    ppermute x5, waiting for transfers between devices, swap_space(): lax.ppermute(values, 'space', [(k, size - 1 - k) for k in range(size)])  13.5 us
    ppermute x5, starting transfers between devices, swap_space(): lax.ppermute(values, 'space', [(k, size - 1 - k) for k in range(size)])  7.21 us
    all_to_all x1, starting transfers between devices, step(): received = lax.all_to_all(packed, 'dp', 0, 0, tiled=True)  6.32 us
    unnamed x23, local copies, waits for them, and re-layouts  2.58 us
  transfers between devices with their start and end apart: 19, of which 9 were waited for; matrix products, arithmetic and copies ran while one was open for 4% of the time, Pallas kernels for 28%

profile of v2, /device:TPU:0, one launch (start us, length us, event | category | flops | bytes accessed | tf_op | source)
XLA Modules:
  0.0 123.1 jit_solution(10046063030171819510)
XLA Ops:
  0.6 0.0 copy-start.6
  0.6 1.1 reshape_squeeze.3
  1.8 3.0 %collective-permute-start = (bf16[1024,256]{1,0:T(8,128)(2,1)S(1)}, bf16[1024,256]{1,0:T(8,128)(2,1)S(1)}, u32[]{:S(2)}, u32[]{:S(2)}) collective-permute-start(bf16[1024,256]{1,0:T(8,128)(2,1)S(1)} %pad.14.map_ref), channel_id=1, source_target_pairs={{0,1},{1,0},{2,3},{3,2},{4,5},{5,4},{6,7},{7,6},{8,9},{9,8},{10,11... | collective-permute-start | bytes 1572872 | tf_op jit(solution)/shard_map/ppermute | solution.py:352
  4.9 0.1 fusion.1
  5.0 0.1 add_bitcast_fusion
  5.2 0.2 copy.12
  5.4 0.0 slice-start
  5.4 0.0 slice-start.1
  5.4 5.7 %shard_map.76 = (bf16[896,1024]{1,0:T(8,128)(2,1)S(1)}, bf16[896,1024]{1,0:T(8,128)(2,1)S(1)}, f32[6272,256]{1,0:T(8,128)S(1)}) custom-call(f32[896,128]{1,0:T(8,128)S(1)} %pad.13.clone.pts, bf16[1024,256]{1,0:T(8,128)(2,1)S(1)} %pad.14.map_ref), custom_call_target="tpu_custom_call" | custom-call | flops 3288334336 | bytes 1048576 | tf_op jit(solution)/shard_map/pallas_call | solution.py:58
  11.1 5.6 %collective-permute-done.map_ref = bf16[1024,256]{1,0:T(8,128)(2,1)S(1)} collective-permute-done((bf16[1024,256]{1,0:T(8,128)(2,1)S(1)}, bf16[1024,256]{1,0:T(8,128)(2,1)S(1)}, u32[]{:S(2)}, u32[]{:S(2)}) %collective-permute-start) | collective-permute-done | bytes 524320 | tf_op jit(solution)/shard_map/ppermute | solution.py:352
  16.8 11.0 %shard_map.77 = (f32[128,256]{1,0:T(8,128)S(1)}, bf16[128,256]{1,0:T(8,128)(2,1)S(1)}, bf16[16,392,128]{2,1,0:T(8,128)(2,1)}) custom-call(bf16[896,1024]{1,0:T(8,128)(2,1)S(1)} %get-tuple-element.16.col_ref, bf16[896,1024]{1,0:T(8,128)(2,1)S(1)} %get-tuple-element.17.row_ref, bf16[1024,256]{1,0:T(8,128)(2,1)S(1)} %collective-permute-done.map_ref, ...), custom_call_target="tpu_custom_call" | custom-call | flops 3288334336 | bytes 1048576 | tf_op jit(solution)/shard_map/pallas_call | solution.py:58
  27.8 6.3 %all-to-all-start = ((bf16[16,392,128]{2,1,0:T(8,128)(2,1)}), bf16[16,392,128]{2,1,0:T(8,128)(2,1)S(1)}, u32[]{:S(2)}, u32[]{:S(2)}) async-start(bf16[16,392,128]{2,1,0:T(8,128)(2,1)} %get-tuple-element.19), calls=%async_computation | async-start | bytes 3211264 | tf_op jit(solution)/shard_map/all_to_all | solution.py:391
  34.2 1.6 %collective-permute-start.2 = (bf16[256,512]{1,0:T(8,128)(2,1)S(1)}, bf16[256,512]{1,0:T(8,128)(2,1)S(1)}, u32[]{:S(2)}, u32[]{:S(2)}) collective-permute-start(bf16[256,512]{1,0:T(8,128)(2,1)S(1)} %copy-done), channel_id=1, source_target_pairs={{0,1},{1,0},{2,3},{3,2},{4,5},{5,4},{6,7},{7,6},{8,9},{9,8},{10,11... | collective-permute-start | bytes 786440 | tf_op jit(solution)/shard_map/ppermute | solution.py:352
  35.7 0.5 collective-permute-start.1
  36.2 0.0 copy-done.5
  36.2 0.1 fusion.up_ref
  36.4 7.0 %collective-permute-done.2.wother_ref = bf16[256,512]{1,0:T(8,128)(2,1)S(1)} collective-permute-done((bf16[256,512]{1,0:T(8,128)(2,1)S(1)}, bf16[256,512]{1,0:T(8,128)(2,1)S(1)}, u32[]{:S(2)}, u32[]{:S(2)}) %collective-permute-start.2) | collective-permute-done | bytes 262176 | tf_op jit(solution)/shard_map/ppermute | solution.py:352
  43.4 0.8 collective-permute-done.1.recv_ref
  44.2 0.8 head.1
  45.1 0.1 collective-permute-start.10
  45.2 1.3 %collective-permute-done.10 = bf16[128,512]{1,0:T(8,128)(2,1)S(1)} collective-permute-done((bf16[128,512]{1,0:T(8,128)(2,1)S(1)}, bf16[128,512]{1,0:T(8,128)(2,1)S(1)}, u32[]{:S(2)}, u32[]{:S(2)}) %collective-permute-start.10) | collective-permute-done | bytes 131104 | tf_op jit(solution)/shard_map/ppermute | solution.py:356
  46.5 1.7 %collective-permute-start.11 = (bf16[64,512]{1,0:T(8,128)(2,1)S(1)}, bf16[64,512]{1,0:T(8,128)(2,1)S(1)}, u32[]{:S(2)}, u32[]{:S(2)}) collective-permute-start(bf16[64,512]{1,0:T(8,128)(2,1)S(1)} %dynamic-slice_convert_fusion.1), channel_id=1, source_target_pairs={{0,4},{2,6},{4,0},{6,2},{8,12},{10,14},{12,8},{14,10},{16,20},{18,... | collective-permute-start | bytes 196616 | tf_op jit(solution)/shard_map/ppermute | solution.py:356
  48.2 1.5 %collective-permute-start.3 = (bf16[1,64,512]{2,1,0:T(8,128)(2,1)S(1)}, bf16[1,64,512]{2,1,0:T(8,128)(2,1)S(1)}, u32[]{:S(2)}, u32[]{:S(2)}) collective-permute-start(bf16[1,64,512]{2,1,0:T(8,128)(2,1)S(1)} %bitcast.46), channel_id=1, source_target_pairs={{0,8},{2,10},{4,12},{6,14},{8,0},{10,2},{12,4},{14,6},{16,24},{18,... | collective-permute-start | bytes 196616 | tf_op jit(solution)/shard_map/ppermute | solution.py:356
  49.7 2.4 %collective-permute-start.4 = (bf16[1,64,512]{2,1,0:T(8,128)(2,1)S(1)}, bf16[1,64,512]{2,1,0:T(8,128)(2,1)S(1)}, u32[]{:S(2)}, u32[]{:S(2)}) collective-permute-start(bf16[1,64,512]{2,1,0:T(8,128)(2,1)S(1)} %bitcast.47), channel_id=1, source_target_pairs={{0,16},{2,18},{4,20},{6,22},{8,24},{10,26},{12,28},{14,30},{16,0},... | collective-permute-start | bytes 196616 | tf_op jit(solution)/shard_map/ppermute | solution.py:356
  52.1 0.6 collective-permute-start.5
  52.6 1.0 collective-permute-done.11
  53.6 0.5 collective-permute-start.12
  54.1 2.4 %collective-permute-start.13 = (bf16[64,512]{1,0:T(8,128)(2,1)S(1)}, bf16[64,512]{1,0:T(8,128)(2,1)S(1)}, u32[]{:S(2)}, u32[]{:S(2)}) collective-permute-start(bf16[64,512]{1,0:T(8,128)(2,1)S(1)} %add_convert_fusion.1), channel_id=1, source_target_pairs={{0,16},{2,18},{4,20},{6,22},{8,24},{10,26},{12,28},{14,30},{16,0},... | collective-permute-start | bytes 196616 | tf_op jit(solution)/shard_map/ppermute | solution.py:356
  56.6 6.2 %collective-permute-done.3 = bf16[1,64,512]{2,1,0:T(8,128)(2,1)S(1)} collective-permute-done((bf16[1,64,512]{2,1,0:T(8,128)(2,1)S(1)}, bf16[1,64,512]{2,1,0:T(8,128)(2,1)S(1)}, u32[]{:S(2)}, u32[]{:S(2)}) %collective-permute-start.3) | collective-permute-done | bytes 65568 | tf_op jit(solution)/shard_map/ppermute | solution.py:356
  62.7 3.8 %collective-permute-start.14 = (bf16[64,512]{1,0:T(8,128)(2,1)S(1)}, bf16[64,512]{1,0:T(8,128)(2,1)S(1)}, u32[]{:S(2)}, u32[]{:S(2)}) collective-permute-start(bf16[64,512]{1,0:T(8,128)(2,1)S(1)} %add_convert_fusion.1), channel_id=1, source_target_pairs={{0,24},{2,26},{4,28},{6,30},{8,16},{10,18},{12,20},{14,22},{16,8},... | collective-permute-start | bytes 196616 | tf_op jit(solution)/shard_map/ppermute | solution.py:356
  66.5 13.7 %collective-permute-done.4 = bf16[1,64,512]{2,1,0:T(8,128)(2,1)S(1)} collective-permute-done((bf16[1,64,512]{2,1,0:T(8,128)(2,1)S(1)}, bf16[1,64,512]{2,1,0:T(8,128)(2,1)S(1)}, u32[]{:S(2)}, u32[]{:S(2)}) %collective-permute-start.4) | collective-permute-done | bytes 65568 | tf_op jit(solution)/shard_map/ppermute | solution.py:356
  80.2 0.0 collective-permute-done.5
  80.3 0.0 copy-start.4
  80.3 1.6 %collective-permute-start.6 = (bf16[4,64,512]{2,1,0:T(8,128)(2,1)S(1)}, bf16[4,64,512]{2,1,0:T(8,128)(2,1)S(1)}, u32[]{:S(2)}, u32[]{:S(2)}) collective-permute-start(bf16[4,64,512]{2,1,0:T(8,128)(2,1)S(1)} %pad_maximum_fusion.refs_0_), channel_id=1, source_target_pairs={{0,4},{2,6},{4,0},{6,2},{8,12},{10,14},{12,8},{14,10},{16,20},{18,... | collective-permute-start | bytes 786440 | tf_op jit(solution)/shard_map/ppermute | solution.py:356
  81.9 0.0 collective-permute-done.12
  81.9 1.2 collective-permute-done.13
  83.0 0.0 collective-permute-done.14
  83.1 1.6 %collective-permute-start.15 = (bf16[64,512]{1,0:T(8,128)(2,1)S(1)}, bf16[64,512]{1,0:T(8,128)(2,1)S(1)}, u32[]{:S(2)}, u32[]{:S(2)}) collective-permute-start(bf16[64,512]{1,0:T(8,128)(2,1)S(1)} %add_convert_fusion), channel_id=1, source_target_pairs={{0,4},{2,6},{4,0},{6,2},{8,12},{10,14},{12,8},{14,10},{16,20},{18,... | collective-permute-start | bytes 196616 | tf_op jit(solution)/shard_map/ppermute | solution.py:356
  84.7 13.1 %shard_map.79 = (bf16[6272,256]{1,0:T(8,128)(2,1)S(1)}, bf16[1008,256]{1,0:T(8,128)(2,1)S(1)}) custom-call(f32[8,896]{1,0:T(8,128)S(1)} %get-tuple-element.39.pts, bf16[128,256]{1,0:T(8,128)(2,1)S(1)} %get-tuple-element.26.delta_ref, bf16[12544,256]{1,0:T(8,128)(2,1)} %weight_hbm.1), custom_call_target="tpu_custom_call" | custom-call | flops 3236954112 | bytes 1048576 | tf_op jit(solution)/shard_map/pallas_call | solution.py:58
  97.8 1.6 %copy-done.1 = bf16[6272,256]{1,0:T(8,128)(2,1)} copy-done((bf16[6272,256]{1,0:T(8,128)(2,1)}, bf16[6272,256]{1,0:T(8,128)(2,1)S(1)}, u32[]{:S(2)}) %copy-start.1) | copy-done | bytes 3211288
  99.4 1.5 %collective-permute-start.17 = (bf16[1008,256]{1,0:T(8,128)(2,1)S(1)}, bf16[1008,256]{1,0:T(8,128)(2,1)S(1)}, u32[]{:S(2)}, u32[]{:S(2)}) collective-permute-start(bf16[1008,256]{1,0:T(8,128)(2,1)S(1)} %get-tuple-element.28), channel_id=1, source_target_pairs={{0,1},{1,0},{2,3},{3,2},{4,5},{5,4},{6,7},{7,6},{8,9},{9,8},{10,11... | collective-permute-start | bytes 1548296 | tf_op jit(solution)/shard_map/ppermute | solution.py:352
  100.9 0.0 copy-done.4
  100.9 0.0 collective-permute-start.7
  100.9 0.0 collective-permute-done.6.refs_1_
  101.0 0.0 copy-start.7
  101.0 0.5 collective-permute-start.8
  101.5 0.0 collective-permute-done.15
  101.5 0.7 pad_maximum_fusion.1
  102.2 0.1 collective-permute-start.16
  102.2 0.2 collective-permute-done.7.refs_2_
  102.5 0.7 copy-done.8
  103.2 0.0 collective-permute-done.8.refs_3_
  103.2 0.0 all-to-all-done.packed_ref
  103.2 4.1 %shard_map.78 = (f32[784,256]{1,0:T(8,128)S(1)}, bf16[784,256]{1,0:T(8,128)(2,1)}) custom-call(s32[1]{0:T(128)} %bitcast.me_ref, bf16[16,392,128]{2,1,0:T(8,128)(2,1)S(1)} %all-to-all-done.packed_ref, bf16[4,64,512]{2,1,0:T(8,128)(2,1)} %copy-done.4, bf16[4,64,512]{2,1,0:T(8,128)(2,1)} %copy-done.7, bf16[4,64,512]{2,1,0:T(8,128)(2,1)} %copy-done.8, ...), custom_call_target="tpu_custom_call" | custom-call | flops 822083584 | bytes 1048576 | tf_op jit(solution)/shard_map/pallas_call | solution.py:58
  107.3 0.6 collective-permute-start.9
  107.9 10.3 %shard_map.80.own_ref = f32[1008,256]{1,0:T(8,128)S(1)} custom-call(f32[8,896]{1,0:T(8,128)S(1)} %get-tuple-element.39.pts, bf16[6272,256]{1,0:T(8,128)(2,1)} %copy-done.1), custom_call_target="tpu_custom_call" | custom-call | flops 3236954112 | bytes 1048576 | tf_op jit(solution)/shard_map/pallas_call | solution.py:58
  118.2 0.0 collective-permute-done.16
  118.2 1.0 broadcast_select_fusion.1
  119.2 0.9 maximum_convert_fusion
  120.0 0.0 collective-permute-done.17.recv_ref
  120.1 0.1 shard_map.81
  120.1 2.0 %broadcast_in_dim_reshape.4 = f32[1,12,84,256]{3,0,2,1:T(1,128)} reshape(f32[1008,256]{1,0:T(8,128)S(1)} %shard_map.81) | data formatting | bytes 2064384 | tf_op jit(solution)/shard_map/broadcast_in_dim;reshape | solution.py:441
  122.2 0.0 collective-permute-done.9
  122.2 1.0 convert_add_fusion
  (32 shorter events, 0.4 us)
Async XLA Ops:
  0.6 4.2 %copy-start.6 = (s32[1,128,4]{1,2,0:T(4,128)S(1)}, s32[1,128,4]{1,2,0:T(4,128)}, u32[]{:S(2)}) copy-start(s32[1,128,4]{1,2,0:T(4,128)} %param.6) | copy-start | bytes 6148
  1.8 15.0 %collective-permute-start = (bf16[1024,256]{1,0:T(8,128)(2,1)S(1)}, bf16[1024,256]{1,0:T(8,128)(2,1)S(1)}, u32[]{:S(2)}, u32[]{:S(2)}) collective-permute-start(bf16[1024,256]{1,0:T(8,128)(2,1)S(1)} %pad.14.map_ref), channel_id=1, source_target_pairs={{0,1},{1,0},{2,3},{3,2},{4,5},{5,4},{6,7},{7,6},{8,9},{9,8},{10,11... | collective-permute-start | bytes 1572872 | tf_op jit(solution)/shard_map/ppermute | solution.py:352
  5.4 11.4 %slice-start = ((s8[6422528]{0:T(1024)(128)(4,1)}), s8[4194304]{0:T(1024)(128)(4,1)S(1)}, s32[]{:S(2)}) async-start(s8[6422528]{0:T(1024)(128)(4,1)} %bitcast.44), calls=%async_computation.1 | async-start | bytes 8388608
  5.4 11.4 %slice-start.1 = ((s8[6422528]{0:T(1024)(128)(4,1)}), s8[2228224]{0:T(1024)(128)(4,1)S(1)}, s32[]{:S(2)}) async-start(s8[6422528]{0:T(1024)(128)(4,1)} %bitcast.44), calls=%async_computation.2 | async-start | bytes 4456448
  27.8 6.3 %copy-start = (bf16[256,512]{1,0:T(8,128)(2,1)S(1)}, bf16[256,512]{1,0:T(8,128)(2,1)}, u32[]{:S(2)}) copy-start(bf16[256,512]{1,0:T(8,128)(2,1)} %wown_ref.1) | copy-start | bytes 786436
  27.8 8.4 %copy-start.5 = (bf16[1,128,512]{2,1,0:T(8,128)(2,1)S(1)}, bf16[1,128,512]{2,1,0:T(8,128)(2,1)}, u32[]{:S(2)}) copy-start(bf16[1,128,512]{2,1,0:T(8,128)(2,1)} %param.9) | copy-start | bytes 393220
  27.8 75.4 %all-to-all-start = ((bf16[16,392,128]{2,1,0:T(8,128)(2,1)}), bf16[16,392,128]{2,1,0:T(8,128)(2,1)S(1)}, u32[]{:S(2)}, u32[]{:S(2)}) async-start(bf16[16,392,128]{2,1,0:T(8,128)(2,1)} %get-tuple-element.19), calls=%async_computation | async-start | bytes 3211264 | tf_op jit(solution)/shard_map/all_to_all | solution.py:391
  34.2 9.2 %collective-permute-start.2 = (bf16[256,512]{1,0:T(8,128)(2,1)S(1)}, bf16[256,512]{1,0:T(8,128)(2,1)S(1)}, u32[]{:S(2)}, u32[]{:S(2)}) collective-permute-start(bf16[256,512]{1,0:T(8,128)(2,1)S(1)} %copy-done), channel_id=1, source_target_pairs={{0,1},{1,0},{2,3},{3,2},{4,5},{5,4},{6,7},{7,6},{8,9},{9,8},{10,11... | collective-permute-start | bytes 786440 | tf_op jit(solution)/shard_map/ppermute | solution.py:352
  35.7 8.5 %collective-permute-start.1 = (bf16[128,256]{1,0:T(8,128)(2,1)S(1)}, bf16[128,256]{1,0:T(8,128)(2,1)S(1)}, u32[]{:S(2)}, u32[]{:S(2)}) collective-permute-start(bf16[128,256]{1,0:T(8,128)(2,1)S(1)} %get-tuple-element.21), channel_id=1, source_target_pairs={{0,1},{1,0},{2,3},{3,2},{4,5},{5,4},{6,7},{7,6},{8,9},{9,8},{10,11... | collective-permute-start | bytes 196616 | tf_op jit(solution)/shard_map/ppermute | solution.py:352
  45.1 1.4 %collective-permute-start.10 = (bf16[128,512]{1,0:T(8,128)(2,1)S(1)}, bf16[128,512]{1,0:T(8,128)(2,1)S(1)}, u32[]{:S(2)}, u32[]{:S(2)}) collective-permute-start(bf16[128,512]{1,0:T(8,128)(2,1)S(1)} %dynamic-slice_convert_fusion), channel_id=1, source_target_pairs={{0,2},{2,0},{4,6},{6,4},{8,10},{10,8},{12,14},{14,12},{16,18},{18,... | collective-permute-start | bytes 393224 | tf_op jit(solution)/shard_map/ppermute | solution.py:356
  46.5 7.1 %collective-permute-start.11 = (bf16[64,512]{1,0:T(8,128)(2,1)S(1)}, bf16[64,512]{1,0:T(8,128)(2,1)S(1)}, u32[]{:S(2)}, u32[]{:S(2)}) collective-permute-start(bf16[64,512]{1,0:T(8,128)(2,1)S(1)} %dynamic-slice_convert_fusion.1), channel_id=1, source_target_pairs={{0,4},{2,6},{4,0},{6,2},{8,12},{10,14},{12,8},{14,10},{16,20},{18,... | collective-permute-start | bytes 196616 | tf_op jit(solution)/shard_map/ppermute | solution.py:356
  48.2 14.5 %collective-permute-start.3 = (bf16[1,64,512]{2,1,0:T(8,128)(2,1)S(1)}, bf16[1,64,512]{2,1,0:T(8,128)(2,1)S(1)}, u32[]{:S(2)}, u32[]{:S(2)}) collective-permute-start(bf16[1,64,512]{2,1,0:T(8,128)(2,1)S(1)} %bitcast.46), channel_id=1, source_target_pairs={{0,8},{2,10},{4,12},{6,14},{8,0},{10,2},{12,4},{14,6},{16,24},{18,... | collective-permute-start | bytes 196616 | tf_op jit(solution)/shard_map/ppermute | solution.py:356
  49.7 30.5 %collective-permute-start.4 = (bf16[1,64,512]{2,1,0:T(8,128)(2,1)S(1)}, bf16[1,64,512]{2,1,0:T(8,128)(2,1)S(1)}, u32[]{:S(2)}, u32[]{:S(2)}) collective-permute-start(bf16[1,64,512]{2,1,0:T(8,128)(2,1)S(1)} %bitcast.47), channel_id=1, source_target_pairs={{0,16},{2,18},{4,20},{6,22},{8,24},{10,26},{12,28},{14,30},{16,0},... | collective-permute-start | bytes 196616 | tf_op jit(solution)/shard_map/ppermute | solution.py:356
  52.1 28.2 %collective-permute-start.5 = (bf16[1,64,512]{2,1,0:T(8,128)(2,1)S(1)}, bf16[1,64,512]{2,1,0:T(8,128)(2,1)S(1)}, u32[]{:S(2)}, u32[]{:S(2)}) collective-permute-start(bf16[1,64,512]{2,1,0:T(8,128)(2,1)S(1)} %bitcast.48), channel_id=1, source_target_pairs={{0,24},{2,26},{4,28},{6,30},{8,16},{10,18},{12,20},{14,22},{16,8},... | collective-permute-start | bytes 196616 | tf_op jit(solution)/shard_map/ppermute | solution.py:356
  53.6 28.2 %collective-permute-start.12 = (bf16[64,512]{1,0:T(8,128)(2,1)S(1)}, bf16[64,512]{1,0:T(8,128)(2,1)S(1)}, u32[]{:S(2)}, u32[]{:S(2)}) collective-permute-start(bf16[64,512]{1,0:T(8,128)(2,1)S(1)} %add_convert_fusion.1), channel_id=1, source_target_pairs={{0,8},{2,10},{4,12},{6,14},{8,0},{10,2},{12,4},{14,6},{16,24},{18,... | collective-permute-start | bytes 196616 | tf_op jit(solution)/shard_map/ppermute | solution.py:356
  54.1 28.9 %collective-permute-start.13 = (bf16[64,512]{1,0:T(8,128)(2,1)S(1)}, bf16[64,512]{1,0:T(8,128)(2,1)S(1)}, u32[]{:S(2)}, u32[]{:S(2)}) collective-permute-start(bf16[64,512]{1,0:T(8,128)(2,1)S(1)} %add_convert_fusion.1), channel_id=1, source_target_pairs={{0,16},{2,18},{4,20},{6,22},{8,24},{10,26},{12,28},{14,30},{16,0},... | collective-permute-start | bytes 196616 | tf_op jit(solution)/shard_map/ppermute | solution.py:356
  62.7 20.3 %collective-permute-start.14 = (bf16[64,512]{1,0:T(8,128)(2,1)S(1)}, bf16[64,512]{1,0:T(8,128)(2,1)S(1)}, u32[]{:S(2)}, u32[]{:S(2)}) collective-permute-start(bf16[64,512]{1,0:T(8,128)(2,1)S(1)} %add_convert_fusion.1), channel_id=1, source_target_pairs={{0,24},{2,26},{4,28},{6,30},{8,16},{10,18},{12,20},{14,22},{16,8},... | collective-permute-start | bytes 196616 | tf_op jit(solution)/shard_map/ppermute | solution.py:356
  80.3 20.7 %copy-start.4 = (bf16[4,64,512]{2,1,0:T(8,128)(2,1)}, bf16[4,64,512]{2,1,0:T(8,128)(2,1)S(1)}, u32[]{:S(2)}) copy-start(bf16[4,64,512]{2,1,0:T(8,128)(2,1)S(1)} %pad_maximum_fusion.refs_0_) | copy-start | bytes 786436
  80.3 20.7 %collective-permute-start.6 = (bf16[4,64,512]{2,1,0:T(8,128)(2,1)S(1)}, bf16[4,64,512]{2,1,0:T(8,128)(2,1)S(1)}, u32[]{:S(2)}, u32[]{:S(2)}) collective-permute-start(bf16[4,64,512]{2,1,0:T(8,128)(2,1)S(1)} %pad_maximum_fusion.refs_0_), channel_id=1, source_target_pairs={{0,4},{2,6},{4,0},{6,2},{8,12},{10,14},{12,8},{14,10},{16,20},{18,... | collective-permute-start | bytes 786440 | tf_op jit(solution)/shard_map/ppermute | solution.py:356
  83.1 18.4 %collective-permute-start.15 = (bf16[64,512]{1,0:T(8,128)(2,1)S(1)}, bf16[64,512]{1,0:T(8,128)(2,1)S(1)}, u32[]{:S(2)}, u32[]{:S(2)}) collective-permute-start(bf16[64,512]{1,0:T(8,128)(2,1)S(1)} %add_convert_fusion), channel_id=1, source_target_pairs={{0,4},{2,6},{4,0},{6,2},{8,12},{10,14},{12,8},{14,10},{16,20},{18,... | collective-permute-start | bytes 196616 | tf_op jit(solution)/shard_map/ppermute | solution.py:356
  97.8 1.6 %copy-start.1 = (bf16[6272,256]{1,0:T(8,128)(2,1)}, bf16[6272,256]{1,0:T(8,128)(2,1)S(1)}, u32[]{:S(2)}) copy-start(bf16[6272,256]{1,0:T(8,128)(2,1)S(1)} %get-tuple-element.27.crop_hbm) | copy-start | bytes 9633796
  99.4 20.6 %collective-permute-start.17 = (bf16[1008,256]{1,0:T(8,128)(2,1)S(1)}, bf16[1008,256]{1,0:T(8,128)(2,1)S(1)}, u32[]{:S(2)}, u32[]{:S(2)}) collective-permute-start(bf16[1008,256]{1,0:T(8,128)(2,1)S(1)} %get-tuple-element.28), channel_id=1, source_target_pairs={{0,1},{1,0},{2,3},{3,2},{4,5},{5,4},{6,7},{7,6},{8,9},{9,8},{10,11... | collective-permute-start | bytes 1548296 | tf_op jit(solution)/shard_map/ppermute | solution.py:352
  100.9 1.5 %collective-permute-start.7 = (bf16[4,64,512]{2,1,0:T(8,128)(2,1)S(1)}, bf16[4,64,512]{2,1,0:T(8,128)(2,1)S(1)}, u32[]{:S(2)}, u32[]{:S(2)}) collective-permute-start(bf16[4,64,512]{2,1,0:T(8,128)(2,1)S(1)} %pad_maximum_fusion.refs_0_), channel_id=1, source_target_pairs={{0,2},{2,0},{4,6},{6,4},{8,10},{10,8},{12,14},{14,12},{16,18},{18,... | collective-permute-start | bytes 786440 | tf_op jit(solution)/shard_map/ppermute | solution.py:356
  101.0 2.2 %copy-start.7 = (bf16[4,64,512]{2,1,0:T(8,128)(2,1)}, bf16[4,64,512]{2,1,0:T(8,128)(2,1)S(1)}, u32[]{:S(2)}) copy-start(bf16[4,64,512]{2,1,0:T(8,128)(2,1)S(1)} %collective-permute-done.6.refs_1_) | copy-start | bytes 786436
  101.0 2.2 %collective-permute-start.8 = (bf16[4,64,512]{2,1,0:T(8,128)(2,1)S(1)}, bf16[4,64,512]{2,1,0:T(8,128)(2,1)}, u32[]{:S(2)}, u32[]{:S(2)}) collective-permute-start(bf16[4,64,512]{2,1,0:T(8,128)(2,1)S(1)} %collective-permute-done.6.refs_1_), channel_id=1, source_target_pairs={{0,2},{2,0},{4,6},{6,4},{8,10},{10,8},{12,14},{14,12},{16,18},{18,... | collective-permute-start | bytes 786440 | tf_op jit(solution)/shard_map/ppermute | solution.py:356
  101.5 1.7 %copy-start.2 = (bf16[64,512]{1,0:T(8,128)(2,1)}, bf16[64,512]{1,0:T(8,128)(2,1)S(1)}, u32[]{:S(2)}) copy-start(bf16[64,512]{1,0:T(8,128)(2,1)S(1)} %get-tuple-element.38) | copy-start | bytes 196612
  102.2 16.1 %collective-permute-start.16 = (bf16[128,512]{1,0:T(8,128)(2,1)}, bf16[128,512]{1,0:T(8,128)(2,1)}, u32[]{:S(2)}, u32[]{:S(2)}) collective-permute-start(bf16[128,512]{1,0:T(8,128)(2,1)} %pad_maximum_fusion.1), channel_id=1, source_target_pairs={{0,2},{2,0},{4,6},{6,4},{8,10},{10,8},{12,14},{14,12},{16,18},{18,... | collective-permute-start | bytes 393224 | tf_op jit(solution)/shard_map/ppermute | solution.py:356
  102.5 0.7 copy-start.8
  107.3 14.8 %collective-permute-start.9 = (bf16[784,256]{1,0:T(8,128)(2,1)}, bf16[784,256]{1,0:T(8,128)(2,1)S(1)}, u32[]{:S(2)}, u32[]{:S(2)}) collective-permute-start(bf16[784,256]{1,0:T(8,128)(2,1)} %get-tuple-element.24), channel_id=1, source_target_pairs={{0,1},{1,0},{2,3},{3,2},{4,5},{5,4},{6,7},{7,6},{8,9},{9,8},{10,11... | collective-permute-start | bytes 1204232 | tf_op jit(solution)/shard_map/ppermute | solution.py:352
  107.9 10.3 %copy-start.3 = (bf16[64,512]{1,0:T(8,128)(2,1)S(1)}, bf16[64,512]{1,0:T(8,128)(2,1)}, u32[]{:S(2)}) copy-start(bf16[64,512]{1,0:T(8,128)(2,1)} %copy-done.2) | copy-start | bytes 196612
